TPU v7x, 32 devices: a whole 2x2x4 slice. The times are simulated.
32 devices in a mesh: space: 4 (over y, core), dev: 8 (over z, x).
Axes of the slice: x: 2, y: 2, z: 4, core: 2. Of those that a mesh axis runs over, the one named last changes fastest.
Arguments:
- density_matrix: float32 [4096, 4096], P(('space', 'dev')), may hold values from -0.2 to 0.2
- basis: float32 [64, 384, 1024], P(('space', 'dev')), may hold values from -1.6 to 1.6
- union: int32 [64, 8], P(('space', 'dev')), may hold values from 0 to 31, as said below
- weights: float32 [64, 384], P(('space', 'dev')), may hold values from 0.2 to 2
- in_scale: float32 [256], replicated, may hold values from 0.3 to 3
- in_shift: float32 [256], replicated, may hold values from -1 to 1
- hidden_weight: float32 [256, 256], replicated, may hold values from -0.375 to 0.375
- hidden_bias: float32 [256], replicated, may hold values from -3 to 3
- out_weight: float32 [256], replicated, may hold values from -0.375 to 0.375
Outputs:
- density: float32 [64, 384], P(('space', 'dev'))
- potential: float32 [4096, 4096], P(('space', 'dev'))
Inputs may be any that keep to these rules, and one draw needn't show every extreme that they name: `union`: row b lists 8 distinct tiles, all among tiles (g - 1) * 8 to (g + 2) * 8 - 1, where g = b // 16.
All inputs are finite; a program needn't handle non-finite values.
Results may differ from a plain program's by a relative error of at most 0.00011.
Values sent between devices are 32-bit elements; how exact they have to be, the bound alone decides.
No kernel may reach another device: no remote copies, remote signals or barrier semaphores. Data moves between devices by JAX's collectives and lax.ppermute only.
A program may use at most 192 MiB of HBM per device.

v0:
```python
import jax
import jax.numpy as jnp
from jax import lax
from jax.sharding import PartitionSpec as P

TILE = 128
U = 8


highest = lax.Precision.HIGHEST


def passed_along(block, axis, distance):
    devices = range(lax.axis_size(axis))
    route = [(i - distance, i) for i in devices if i - distance in devices]
    return lax.ppermute(block, axis, route)


def potential_net(point_rho, in_scale, in_shift, hidden_weight, hidden_bias, out_weight):
    first_layer = jnp.tanh(point_rho[:, None] * in_scale[None, :] + in_shift[None, :])
    pre_act = (
        jnp.dot(first_layer, hidden_weight, precision=highest, preferred_element_type=jnp.float32)
        + hidden_bias[None, :]
    )
    second = jax.nn.silu(pre_act)
    return jnp.dot(second, out_weight, precision=highest, preferred_element_type=jnp.float32)


def place_columns(piece_block, centre, region, orbitals):
    canvas = jnp.zeros((piece_block.shape[0], orbitals + 2 * region), jnp.float32)
    canvas = lax.dynamic_update_slice_in_dim(canvas, piece_block, centre * region, 1)
    return canvas[:, region : region + orbitals]


def on_device(
    density_matrix,
    basis,
    union,
    weights,
    in_scale,
    in_shift,
    hidden_weight,
    hidden_bias,
    out_weight,
):
    row_count, orbitals = density_matrix.shape
    space_count = lax.axis_size("space")
    region = orbitals // space_count
    window_cols = 3 * region
    region_tiles = region // TILE
    group_index = lax.axis_index("space")
    padded = jnp.pad(density_matrix, ((0, 0), (region, region)))
    own_rows = lax.dynamic_slice_in_dim(padded, group_index * region, window_cols, 1)
    upward = lax.dynamic_slice_in_dim(padded, (group_index + 1) * region, window_cols, 1)
    downward = lax.dynamic_slice_in_dim(padded, (group_index - 1) * region, window_cols, 1)
    from_below = passed_along(upward, "space", 1)
    from_above = passed_along(downward, "space", -1)
    stacked = jnp.stack([from_below, own_rows, from_above])
    window = lax.all_gather(stacked, "dev", axis=1, tiled=True)
    blocks = window.reshape(3 * region_tiles, TILE, 3 * region_tiles, TILE)
    first_tile = (group_index - 1) * region_tiles
    partial_value = jnp.zeros_like(blocks)
    densities = []
    for batch_index in range(basis.shape[0]):
        values = basis[batch_index]
        union_width = values.shape[1]
        chosen = union[batch_index] - first_tile
        sub_block = blocks[chosen[:, None], :, chosen[None, :], :]
        sub_block = sub_block.transpose(0, 2, 1, 3).reshape(union_width, union_width)
        projected = jnp.dot(
            values, sub_block, precision=highest, preferred_element_type=jnp.float32
        )
        point_rho = jnp.sum(projected * values, axis=1)
        point_pot = potential_net(
            point_rho, in_scale, in_shift, hidden_weight, hidden_bias, out_weight
        )
        scaled = values * (weights[batch_index] * point_pot)[:, None]
        product = lax.dot_general(
            scaled,
            values,
            (((0,), (0,)), ((), ())),
            precision=highest,
            preferred_element_type=jnp.float32,
        )
        term_tile = product.reshape(U, TILE, U, TILE).transpose(0, 2, 1, 3)
        partial_value = partial_value.at[chosen[:, None], :, chosen[None, :], :].add(term_tile)
        densities.append(point_rho)
    density = jnp.stack(densities)
    partial_value = partial_value.reshape(3, region, window_cols)
    down_block = passed_along(partial_value[0], "space", -1)
    up_block = passed_along(partial_value[2], "space", 1)
    full_rows = place_columns(partial_value[1], group_index, region, orbitals)
    full_rows = full_rows + place_columns(down_block, group_index + 1, region, orbitals)
    full_rows = full_rows + place_columns(up_block, group_index - 1, region, orbitals)
    potential = lax.psum_scatter(full_rows, "dev", scatter_dimension=0, tiled=True)
    return (density, potential)


def solution(mesh):
    in_specs = (
        P(("space", "dev"), None),
        P(("space", "dev"), None, None),
        P(("space", "dev"), None),
        P(("space", "dev"), None),
        P(),
        P(),
        P(),
        P(),
        P(),
    )
    out_specs = (P(("space", "dev"), None), P(("space", "dev"), None))
    return jax.shard_map(
        on_device, mesh=mesh, in_specs=in_specs, out_specs=out_specs, check_vma=False
    )
```

profile of v0, /device:TPU:0, one launch (start us, length us, event | category | flops | bytes accessed | tf_op | source)
XLA Modules:
  0.0 1460.3 jit_solution(13159190179048682887)
XLA Ops:
  11.2 3.4 collective-permute-start
  17.5 2.7 pad_maximum_fusion
  26.1 3.1 copy.31
  29.5 726.2 %all-gather.2.cloned.1.call-done = f32[3,1024,3072]{2,1,0:T(8,128)} async-done(((f32[3,128,3072]{2,1,0:T(8,128)}), f32[3,1024,3072]{2,1,0:T(8,128)}) %all-gather.2.cloned.1.call-update) | async-done | bytes 37748752 | tf_op jit(solution)/shard_map/all_gather | solution.py:59
  755.7 19.3 %copy.33 = f32[384,8,24,128]{3,2,1,0:T(8,128)S(1)} copy(f32[384,8,24,128]{3,1,2,0:T(8,128)} %bitcast.142) | data formatting | bytes 75497472
  775.1 15.7 %copy.20 = f32[24,128,24,128]{3,1,2,0:T(8,128)} copy(f32[24,128,24,128]{3,2,1,0:T(8,128)S(1)} %bitcast.138) | data formatting | bytes 75497472 | tf_op jit(solution)/shard_map/reshape | solution.py:60
  790.8 5.0 gather_fusion.1
  795.8 6.5 copy.24
  802.3 4.9 gather_fusion
  807.2 4.7 copy.21
  812.0 13.5 fusion.10
  827.8 13.7 fusion.9
  842.7 8.7 fusion.51
  851.4 8.6 fusion.52
  860.0 12.6 broadcast_in_dim.20
  872.6 14.1 scatter_fusion
  886.7 14.2 scatter_fusion.1
  900.9 27.3 %fusion.49 = (f32[8,128,24,128]{3,1,2,0:T(8,128)}, f32[8,128,24,128]{3,1,2,0:T(8,128)}, f32[8,128,24,128]{3,1,2,0:T(8,128)}) fusion(f32[24,128,24,128]{3,1,2,0:T(8,128)} %scatter_fusion.1), kind=kLoop, calls=%fused_computation.85 | loop fusion | bytes 75497472 | tf_op jit(solution)/shard_map/slice | solution.py:92
  928.1 16.2 %copy.28 = f32[8,128,24,128]{3,2,1,0:T(8,128)} copy(f32[8,128,24,128]{3,1,2,0:T(8,128)} %get-tuple-element.9) | data formatting | bytes 25165824 | tf_op jit(solution)/shard_map/slice | solution.py:91
  944.3 12.0 copy.54
  956.4 6.8 collective-permute-start.3
  963.1 16.2 %copy.27 = f32[8,128,24,128]{3,2,1,0:T(8,128)} copy(f32[8,128,24,128]{3,1,2,0:T(8,128)} %get-tuple-element.10) | data formatting | bytes 25165824 | tf_op jit(solution)/shard_map/slice | solution.py:90
  979.3 12.1 copy.55
  992.9 16.2 %copy.26 = f32[8,128,24,128]{3,2,1,0:T(8,128)} copy(f32[8,128,24,128]{3,1,2,0:T(8,128)} %get-tuple-element.8) | data formatting | bytes 25165824 | tf_op jit(solution)/shard_map/slice | solution.py:92
  1009.1 11.5 broadcast.78.clone.2
  1020.6 12.4 bitcast_dynamic-update-slice_fusion
  1033.0 11.5 broadcast.78.clone
  1044.5 10.7 constant_dynamic-update-slice_fusion
  1055.2 11.5 broadcast.78.clone.1
  1066.7 10.8 constant_dynamic-update-slice_fusion.1
  1077.4 23.3 %slice_add_fusion = f32[1024,4096]{1,0:T(8,128)} fusion(f32[1024,6144]{1,0:T(8,128)} %constant_dynamic-update-slice_fusion, f32[1024,6144]{1,0:T(8,128)} %constant_dynamic-update-slice_fusion.1, f32[1024,6144]{1,0:T(8,128)} %bitcast_dynamic-update-slice_fusion), kind=kLoop, calls=%fused_computation.4 | loop fusion | flops 8388608 | bytes 67108864 | tf_op jit(solution)/shard_map/add | solution.py:94
  1101.4 351.8 %reduce-scatter.2.cloned.1.call-done = f32[128,4096]{1,0:T(8,128)} async-done(((f32[1024,4096]{1,0:T(8,128)}), f32[128,4096]{1,0:T(8,128)}) %reduce-scatter.2.cloned.1.call-update) | async-done | bytes 2097168 | tf_op jit(solution)/shard_map/reduce_scatter | solution.py:95
  (58 shorter events, 18.5 us)
Async XLA Ops:
  7.2 818.4 %copy-start = (f32[256,256]{1,0:T(8,128)S(1)}, f32[256,256]{1,0:T(8,128)}, u32[]{:S(2)}) copy-start(f32[256,256]{1,0:T(8,128)} %param.15) | copy-start | bytes 786436
  7.2 748.6 %all-gather.2.cloned.1.call-start = ((), (), s32[]{:S(2)}) async-start(), calls=%async_computation.1 | async-start | bytes 42467328 | tf_op jit(solution)/shard_map/all_gather | solution.py:59
  9.9 5.6 collective-permute-start.1
  11.2 6.3 collective-permute-start
  20.2 1.9 copy-start.4
  20.2 5.7 copy-start.10
  20.2 1433.0 %reduce-scatter.2.cloned.1.call-start = ((), (), s32[]{:S(2)}) async-start(), calls=%async_computation.2 | async-start | bytes 18874368 | tf_op jit(solution)/shard_map/reduce_scatter | solution.py:95
  24.0 5.5 copy-start.9
  807.2 4.7 copy-start.2
  807.2 4.7 copy-start.5
  812.0 13.6 copy-start.6
  812.0 13.6 copy-start.7
  812.0 13.6 copy-start.8
  812.0 14.1 copy-start.11
  825.6 2.2 copy-start.3
  956.4 76.6 %collective-permute-start.3 = (f32[1024,3072]{1,0:T(8,128)}, f32[1024,3072]{1,0:T(8,128)}, u32[]{:S(2)}, u32[]{:S(2)}) collective-permute-start(f32[1024,3072]{1,0:T(8,128)} %bitcast.152), channel_id=1, source_target_pairs={{0,8},{8,16},{16,24},{1,9},{9,17},{17,25},{2,10},{10,18},{18,26},{... | collective-permute-start | bytes 37748744 | tf_op jit(solution)/shard_map/ppermute | solution.py:16
  991.4 63.8 %collective-permute-start.2 = (f32[1024,3072]{1,0:T(8,128)}, f32[1024,3072]{1,0:T(8,128)}, u32[]{:S(2)}, u32[]{:S(2)}) collective-permute-start(f32[1024,3072]{1,0:T(8,128)} %bitcast.151), channel_id=1, source_target_pairs={{8,0},{16,8},{24,16},{9,1},{17,9},{25,17},{10,2},{18,10},{26,18},{... | collective-permute-start | bytes 37748744 | tf_op jit(solution)/shard_map/ppermute | solution.py:16
  1100.8 352.5 %copy-start.1 = (f32[256,256]{1,0:T(8,128)S(1)}, f32[256,256]{1,0:T(8,128)}, u32[]{:S(2)}) copy-start(f32[256,256]{1,0:T(8,128)} %param.15) | copy-start | bytes 786436
Sparse Core Ops, SparseCore 0:
  20.3 735.3 all-gather.1
  1100.9 352.3 reduce-scatter.1
where the time goes:
time: 1470 us; the launch traced here: 1460 us
  waiting for transfers between devices  1080 us (73%)
  local copies, waits for them, and re-layouts  250 us (17%)
  other arithmetic  55.2 us (4%)
  matrix products  46.8 us (3%)
    all_gather x1, waiting for transfers between devices, on_device(): window = lax.all_gather(stacked, 'dev', axis=1, tiled=True)  726 us
    reduce_scatter x1, waiting for transfers between devices, on_device(): lax.psum_scatter(full_rows, 'dev', scatter_dimension=0, tiled=True)  352 us
    unnamed x29, local copies, waits for them, and re-layouts  51.2 us
    slice x2, local copies, waits for them, and re-layouts, on_device(): full_rows = place_columns(partial_value[1], group_index, region, orbitals)  43.5 us
    another operation x3, local copies, waits for them, and re-layouts  34.4 us
    dynamic_update_slice x3, local copies, waits for them, and re-layouts, place_columns(): lax.dynamic_update_slice_in_dim(canvas, piece_block, centre * region, 1)  33.9 us
  transfers between devices with their start and end apart: 6, of which 4 were waited for; matrix products, arithmetic and copies ran while one was open for 7% of the time, Pallas kernels for 0%

commit v1 on v0

--- a/solution.py
+++ b/solution.py
@@ -1,6 +1,11 @@
+import functools
+
 import jax
 import jax.numpy as jnp
 from jax import lax
+from jax.experimental import pallas as pl
+from jax.experimental.pallas import tpu as pltpu
+
 from jax.sharding import PartitionSpec as P
 
 TILE = 128
@@ -32,7 +37,7 @@
     return canvas[:, region : region + orbitals]
 
 
-def on_device(
+def by_window(
     density_matrix,
     basis,
     union,
@@ -43,7 +48,7 @@
     hidden_bias,
     out_weight,
 ):
-    row_count, orbitals = density_matrix.shape
+    _, orbitals = density_matrix.shape
     space_count = lax.axis_size("space")
     region = orbitals // space_count
     window_cols = 3 * region
@@ -96,6 +101,367 @@
     return (density, potential)
 
 
+QUAD = 4
+NT = (((1,), (1,)), ((), ()))
+NN = (((1,), (0,)), ((), ()))
+
+
+def split(value):
+    high = value.astype(jnp.bfloat16)
+    return high, (value - high.astype(jnp.float32)).astype(jnp.bfloat16)
+
+
+def product(a, b, dims):
+    return lax.dot_general(a, b, dims, preferred_element_type=jnp.float32)
+
+
+def tile_at(index):
+    return pl.ds(pl.multiple_of(index * TILE, TILE), TILE)
+
+
+def place_of(tile, where, region_tiles):
+    quads = region_tiles // QUAD
+    mine = tile % QUAD == where[1]
+    turn = (tile % region_tiles // QUAD - where[2] + quads) % quads
+    return mine, turn, tile // region_tiles - where[0] + 1
+
+
+def density_kernel(pieces, first, n_rows, region_tiles, where, union, *refs):
+    n_x = len(pieces)
+    x_refs, row_refs = refs[:n_x], refs[n_x : n_x + n_rows]
+    rho_ref, high_ref, low_ref, x_full, d_both, total = refs[-6:]
+    step = pl.program_id(0)
+    for x_ref, (start, count, point) in zip(x_refs, pieces, strict=True):
+
+        @pl.when((step >= start) & (step < start + count))
+        def _():
+            value = x_ref[0]
+            at = pl.ds(point, x_ref.shape[1])
+            x_full[at, :] = value
+            high_ref[0, at, :], low_ref[0, at, :] = split(value)
+
+    total[...] = jnp.zeros_like(total)
+    base = (first + step) * U
+
+    @pl.loop(0, U)
+    def _(i):
+        mine, turn, place = place_of(union[base + i], where, region_tiles)
+
+        @pl.when(mine)
+        def _():
+            for n in range(n_rows):
+
+                @pl.when(turn * 3 + place == n)
+                def _():
+                    for j in range(U):
+                        high, low = split(row_refs[n][:, tile_at(union[base + j])])
+                        d_both[:TILE, j * TILE : (j + 1) * TILE] = high
+                        d_both[TILE:, j * TILE : (j + 1) * TILE] = low
+
+            both = product(high_ref[0], d_both[...], NT)
+            row = both[:, :TILE] + (both[:, TILE:] + product(low_ref[0], d_both[:TILE], NT))
+            total[...] += row * x_full[:, tile_at(i)]
+
+    ones = jnp.ones((8, TILE), jnp.float32)
+    rho_ref[0] = lax.dot_general(
+        ones, total[...], NT, precision=highest, preferred_element_type=jnp.float32
+    )[:1]
+
+
+def potential_kernel(
+    k, places, chunks, region_tiles, where, union, high_ref, low_ref, scale_ref, *refs
+):
+    out_refs, sums, term = refs[:-2], refs[-2], refs[-1]
+    step = pl.program_id(0)
+
+    @pl.when(step == 0)
+    def _():
+        sums[...] = jnp.zeros_like(sums)
+
+    @pl.loop(0, U)
+    def _(i):
+        mine, turn, place = place_of(union[step * U + i], where, region_tiles)
+        wanted = functools.reduce(jnp.logical_or, [place == r for r in places])
+
+        @pl.when(mine & (turn == k) & wanted)
+        def _():
+            here = tile_at(i)
+            value = high_ref[0, :, here].astype(jnp.float32) + low_ref[0, :, here].astype(
+                jnp.float32
+            )
+            high, low = split(value.T * scale_ref[0])
+            both = product(jnp.concatenate([high, low]), high_ref[0], NN)
+            term[...] = both[:TILE] + (both[TILE:] + product(high, low_ref[0], NN))
+            slot = 0 if len(places) == 1 else sum((place == r) * n for n, r in enumerate(places))
+            for j in range(U):
+                at = tile_at(union[step * U + j])
+                sums[slot, :, at] += term[:, j * TILE : (j + 1) * TILE]
+
+    @pl.when(step == pl.num_programs(0) - 1)
+    def _():
+        for n in range(len(places)):
+            for c, (first, last) in enumerate(chunks):
+                out_refs[n * len(chunks) + c][...] = sums[n, :, first:last]
+
+
+def joined_kernel(chunks, *refs):
+    out_ref, refs = refs[-1], refs[:-1]
+    terms = len(refs) // len(chunks)
+    for c, (first, last) in enumerate(chunks):
+        value = refs[c][...]
+        for n in range(1, terms):
+            value = value + refs[n * len(chunks) + c][...]
+        out_ref[:, first:last] = value
+
+
+def net_kernel(rho_ref, weight_ref, scale_ref, shift_ref, hidden_ref, bias_ref, out_w_ref, out_ref):
+    h_high, h_low = split(hidden_ref[...])
+    for b in range(rho_ref.shape[0]):
+        first_layer = jnp.tanh(rho_ref[b] * scale_ref[...] + shift_ref[...])
+        f_high, f_low = split(first_layer)
+        pre_act = (
+            product(h_high, f_high, NN)
+            + (product(h_high, f_low, NN) + product(h_low, f_high, NN))
+            + bias_ref[...]
+        )
+        second = pre_act / (1.0 + jnp.exp(-pre_act))
+        out_ref[b] = jnp.sum(out_w_ref[...] * second, axis=0, keepdims=True) * weight_ref[b]
+
+
+def call_density(xs, pieces, rows, where, union, region_tiles, first, filled, whole):
+    _, points, width = whole
+    steps = max(start + count for start, count, _ in pieces)
+
+    def x_spec(x, start, count):
+        return pl.BlockSpec(
+            (1, *x.shape[1:]), lambda g, *_: (jnp.clip(g - start, 0, count - 1), 0, 0)
+        )
+
+    row_spec = pl.BlockSpec(rows[0].shape, lambda g, *_: (0, 0), pipeline_mode=pl.Buffered(1))
+    halves = jax.ShapeDtypeStruct(whole, jnp.bfloat16)
+    half_spec = pl.BlockSpec((1, points, width), lambda g, *_: (first + g, 0, 0))
+    n_in = 2 + len(xs) + len(rows)
+    return pl.pallas_call(
+        functools.partial(density_kernel, pieces, first, len(rows), region_tiles),
+        out_shape=[jax.ShapeDtypeStruct((steps, 1, points), jnp.float32), halves, halves],
+        grid_spec=pltpu.PrefetchScalarGridSpec(
+            num_scalar_prefetch=2,
+            grid=(steps,),
+            in_specs=[
+                x_spec(x, start, count) for x, (start, count, _) in zip(xs, pieces, strict=True)
+            ]
+            + [row_spec] * len(rows)
+            + [pl.BlockSpec(memory_space=pl.ANY)] * len(filled),
+            out_specs=[
+                pl.BlockSpec((1, 1, points), lambda g, *_: (g, 0, 0)),
+                half_spec,
+                half_spec,
+            ],
+            scratch_shapes=[
+                pltpu.VMEM((points, width), jnp.float32),
+                pltpu.VMEM((2 * TILE, width), jnp.bfloat16),
+                pltpu.VMEM((points, TILE), jnp.float32),
+            ],
+        ),
+        input_output_aliases={n_in + n: 1 + n for n in range(len(filled))},
+        cost_estimate=pl.CostEstimate(
+            flops=6 * steps * points * width * width // QUAD,
+            bytes_accessed=8 * steps * points * width + sum(r.size for r in rows) * 4,
+            transcendentals=0,
+        ),
+        name="density_rows",
+    )(where, union, *xs, *rows, *filled)
+
+
+def call_potential(high, low, scale, k, places, chunks, where, union, region_tiles):
+    batches, points, width = high.shape
+    widths = [last - first for first, last in chunks] * len(places)
+    half_spec = pl.BlockSpec((1, points, width), lambda g, *_: (g, 0, 0))
+    return pl.pallas_call(
+        functools.partial(potential_kernel, k, places, chunks, region_tiles),
+        out_shape=[jax.ShapeDtypeStruct((TILE, w), jnp.float32) for w in widths],
+        grid_spec=pltpu.PrefetchScalarGridSpec(
+            num_scalar_prefetch=2,
+            grid=(batches,),
+            in_specs=[
+                half_spec,
+                half_spec,
+                pl.BlockSpec((1, 1, points), lambda g, *_: (g, 0, 0)),
+            ],
+            out_specs=[
+                pl.BlockSpec((TILE, w), lambda g, *_: (0, 0), pipeline_mode=pl.Buffered(1))
+                for w in widths
+            ],
+            scratch_shapes=[
+                pltpu.VMEM((len(places), TILE, chunks[-1][1]), jnp.float32),
+                pltpu.VMEM((TILE, width), jnp.float32),
+            ],
+        ),
+        cost_estimate=pl.CostEstimate(
+            flops=2 * len(places) * batches * points * width * width // QUAD,
+            bytes_accessed=4 * high.size + 4 * len(places) * TILE * chunks[-1][1],
+            transcendentals=0,
+        ),
+        name="potential_rows",
+    )(where, union, high, low, scale)
+
+
+def call_joined(terms, chunks):
+    rows = 4
+    height = TILE // rows
+    widths = [last - first for first, last in chunks]
+    flat = [block for term in terms for block in term]
+    return pl.pallas_call(
+        functools.partial(joined_kernel, chunks),
+        out_shape=jax.ShapeDtypeStruct((TILE, chunks[-1][1]), jnp.float32),
+        grid=(rows,),
+        in_specs=[pl.BlockSpec((height, w), lambda g: (g, 0)) for w in widths] * len(terms),
+        out_specs=pl.BlockSpec((height, chunks[-1][1]), lambda g: (g, 0)),
+        cost_estimate=pl.CostEstimate(
+            flops=TILE * chunks[-1][1] * len(terms),
+            bytes_accessed=4 * TILE * chunks[-1][1] * (len(terms) + 1),
+            transcendentals=0,
+        ),
+        name="joined_rows",
+    )(*flat)
+
+
+def column_groups(regions):
+    meets = [tuple(r for r in range(regions) if abs(r - c) <= 2) for c in range(regions)]
+    groups = []
+    for c in range(regions):
+        if groups and meets[c] == groups[-1][2]:
+            groups[-1] = (groups[-1][0], c + 1, meets[c])
+        else:
+            groups.append((c, c + 1, meets[c]))
+    return groups
+
+
+def by_quads(
+    density_matrix,
+    basis,
+    union,
+    weights,
+    in_scale,
+    in_shift,
+    hidden_weight,
+    hidden_bias,
+    out_weight,
+):
+    orbitals = density_matrix.shape[1]
+    batches, points, width = basis.shape
+    n_dev = lax.axis_size("dev")
+    region_tiles = orbitals // lax.axis_size("space") // TILE
+    quads = n_dev // QUAD
+    space_index, dev_index = lax.axis_index("space"), lax.axis_index("dev")
+    where = jnp.stack([space_index, dev_index % QUAD, dev_index // QUAD])
+
+    def swapped(block, flip):
+        return lax.ppermute(block, "dev", [(d, d ^ flip) for d in range(n_dev)])
+
+    def turned(block, k):
+        route = [(d, (d + QUAD * k) % n_dev) for d in range(n_dev)]
+        return lax.ppermute(block, "dev", route)
+
+    def to_space(block, distance):
+        return passed_along(block, "space", distance)
+
+    bases = [density_matrix]
+    bases += [turned(density_matrix, -k) for k in range(1, quads)]
+    beside = swapped(basis, 1)
+    across = [swapped(basis[b : b + 1], 2) for b in range(batches)]
+    last, middle = batches - 1, 2 * points // 3 // 16 * 16
+    corner = [swapped(across[b], 1) for b in range(last)]
+    corner.append(swapped(across[last][:, :middle], 1))
+    corner.append(swapped(beside[last:, middle:], 2))
+
+    small = jnp.concatenate([weights, union.astype(jnp.float32)], axis=1)
+    small = jnp.pad(small, ((0, 0), (0, -small.shape[1] % TILE)))
+    small = [small] + [swapped(small, flip) for flip in range(1, QUAD)]
+    small = jnp.concatenate(small)
+    all_weights = small[:, :points].reshape(-1, 1, points)
+    tiles = small[:, points : points + U].astype(jnp.int32).reshape(-1)
+
+    rows = []
+    for base in bases:
+        rows += [to_space(base, 1), base, to_space(base, -1)]
+    whole = (QUAD * batches, points, width)
+    early = [basis, beside, *across]
+    early_pieces = [(0, batches, 0), (batches, batches, 0)]
+    early_pieces += [(2 * batches + b, 1, 0) for b in range(batches)]
+    late_pieces = [(b, 1, 0) for b in range(last)] + [(last, 1, 0), (last, 1, middle)]
+    rho_early, high, low = call_density(
+        early, early_pieces, rows, where, tiles, region_tiles, 0, [], whole
+    )
+    rho_late, high, low = call_density(
+        corner, late_pieces, rows, where, tiles, region_tiles, 3 * batches, [high, low], whole
+    )
+    part = jnp.concatenate([rho_early, rho_late]).reshape(2, 2, batches, points)
+    rho = (part + swapped(part, 1)[:, ::-1]) + (
+        swapped(part, 2)[::-1] + swapped(part, 3)[::-1, ::-1]
+    )
+    density = rho[0, 0]
+
+    scale = pl.pallas_call(
+        net_kernel,
+        out_shape=jax.ShapeDtypeStruct(all_weights.shape, jnp.float32),
+        name="potential_net",
+    )(
+        rho.reshape(-1, 1, points),
+        all_weights,
+        in_scale[:, None],
+        in_shift[:, None],
+        hidden_weight.T,
+        hidden_bias[:, None],
+        out_weight[:, None],
+    )
+
+    regions = lax.axis_size("space")
+    groups = column_groups(regions)
+    chunks = tuple((c * orbitals // regions, end * orbitals // regions) for c, end, _ in groups)
+    order = sorted(range(len(groups)), key=lambda n: groups[n][0] - groups[n][1])
+
+    def part_rows(k, places):
+        parts = call_potential(high, low, scale, k, places, chunks, where, tiles, region_tiles)
+        return [parts[n : n + len(chunks)] for n in range(0, len(parts), len(chunks))]
+
+    def piece_to_space(block, n, distance):
+        first, last, _ = groups[n]
+        route = [
+            (r, r + distance)
+            for r in range(regions)
+            if 0 <= r + distance < regions and first - 1 <= r <= last
+        ]
+        return lax.ppermute(block, "space", route)
+
+    def piece_turned(block, n, k):
+        route = [
+            (r * n_dev + d, r * n_dev + (d + QUAD * k) % n_dev)
+            for r in groups[n][2]
+            for d in range(n_dev)
+        ]
+        return lax.ppermute(block, ("space", "dev"), route)
+
+    terms = []
+    for k in [*range(1, quads), 0]:
+        below, above = part_rows(k, (0, 2))
+        received = [None] * len(chunks)
+        for n in order:
+            received[n] = (piece_to_space(below[n], n, -1), piece_to_space(above[n], n, 1))
+        (inner,) = part_rows(k, (1,))
+        if k:
+            terms.append(
+                [
+                    piece_turned(inner[n] + received[n][0] + received[n][1], n, k)
+                    for n in range(len(chunks))
+                ]
+            )
+        else:
+            terms += [inner, [pair[0] for pair in received], [pair[1] for pair in received]]
+    potential = call_joined(terms, chunks)
+    return (density, potential)
+
+
 def solution(mesh):
     in_specs = (
         P(("space", "dev"), None),
@@ -109,6 +475,22 @@
         P(),
     )
     out_specs = (P(("space", "dev"), None), P(("space", "dev"), None))
-    return jax.shard_map(
-        on_device, mesh=mesh, in_specs=in_specs, out_specs=out_specs, check_vma=False
-    )
+    devices = mesh.shape["space"] * mesh.shape["dev"]
+
+    def whole_tile(density_matrix):
+        return density_matrix.shape[0] == devices * TILE and mesh.shape["dev"] % QUAD == 0
+
+    def mapped(plan):
+        return jax.shard_map(
+            plan, mesh=mesh, in_specs=in_specs, out_specs=out_specs, check_vma=False
+        )
+
+    def step(density_matrix, basis, *others):
+        if not whole_tile(density_matrix):
+            return mapped(by_window)(density_matrix, basis, *others)
+
+        return mapped(by_quads)(
+            density_matrix, basis, *others
+        )
+
+    return step

time: 1470 us -> 383 us (0.26)
  waiting for transfers between devices: 1080 us -> 185 us
  local copies, waits for them, and re-layouts: 250 us -> 12.4 us
  Pallas kernels: 0 us -> 88 us
  starting transfers between devices: 13 us -> 85 us
  other arithmetic: 55.2 us -> 6.7 us
  matrix products: 46.8 us -> 0 us
    all_gather x1 -> x0, waiting for transfers between devices: 726 us -> none  [on_device(): window = lax.all_gather(stacked, 'dev', axis=1, tiled=True)]
    reduce_scatter x1 -> x0, waiting for transfers between devices: 352 us -> none  [on_device(): lax.psum_scatter(full_rows, 'dev', scatter_dimension=0, tiled=True)]
    ppermute x0 -> x28, waiting for transfers between devices: none -> 185 us  [the longest x12 129 us: swapped(): return lax.ppermute(block, 'dev', [(d, d ^ flip) for d in range(n_dev)])]
    pallas_call x0 -> x8, Pallas kernels: none -> 88 us  [the longest x4 45.3 us: call_potential(): pl.pallas_call(functools.partial(potential_kernel, k, places, chunks, reg...]
    ppermute x0 -> x28, starting transfers between devices: none -> 74.3 us  [the longest x12 52.7 us: piece_to_space(): return lax.ppermute(block, 'space', route)]
    slice x6 -> x3, local copies, waits for them, and re-layouts: 77.8 us -> 4.01 us  [the longest x1 2.1 us: by_quads(): across = [swapped(basis[b:b + 1], 2) for b in range(batches)]]
    unnamed x29 -> x41, local copies, waits for them, and re-layouts: 51.2 us -> 2.83 us
    dot_general x8 -> x0, matrix products: 46.8 us -> none  [the longest x2 27.3 us: on_device(): jnp.dot(values, sub_block, precision=highest, preferred_element_type=jnp....]
  transfers between devices with their start and end apart: 6 -> 32, of which waited for: 4 -> 6; matrix products, arithmetic and copies ran while one was open for 7% -> 4% of each run, Pallas kernels for 0% -> 15%
where the time goes in v1:
time: 383 us; the launch traced here: 378 us
  waiting for transfers between devices  185 us (48%)
  Pallas kernels  88 us (23%)
  starting transfers between devices  85 us (22%)
  local copies, waits for them, and re-layouts  12.4 us (3%)
  other arithmetic  6.7 us (2%)
    ppermute x12, waiting for transfers between devices, swapped(): return lax.ppermute(block, 'dev', [(d, d ^ flip) for d in range(n_dev)])  129 us
    ppermute x3, waiting for transfers between devices, piece_turned(): return lax.ppermute(block, ('space', 'dev'), route)  56.4 us
    ppermute x12, starting transfers between devices, piece_to_space(): return lax.ppermute(block, 'space', route)  52.7 us
    pallas_call x4, Pallas kernels, call_potential(): pl.pallas_call(functools.partial(potential_kernel, k, places, chunks, reg...  45.3 us
    pallas_call x2, Pallas kernels, call_density(): pl.pallas_call(functools.partial(density_kernel, pieces, first, len(rows)...  33.5 us
    ppermute x12, starting transfers between devices, swapped(): return lax.ppermute(block, 'dev', [(d, d ^ flip) for d in range(n_dev)])  11.1 us
    ppermute x4, starting transfers between devices, passed_along(): return lax.ppermute(block, axis, route)  10.7 us
  transfers between devices with their start and end apart: 32, of which 6 were waited for; matrix products, arithmetic and copies ran while one was open for 4% of the time, Pallas kernels for 15%

profile of v1, /device:TPU:0, one launch (start us, length us, event | category | flops | bytes accessed | tf_op | source)
XLA Modules:
  0.0 378.2 jit_solution(6534617415659688933)
XLA Ops:
  0.7 4.1 %collective-permute-start.8 = (f32[128,4096]{1,0:T(8,128)}, f32[128,4096]{1,0:T(8,128)}, u32[]{:S(2)}, u32[]{:S(2)}) collective-permute-start(f32[128,4096]{1,0:T(8,128)} %refs_4_.1), channel_id=1, source_target_pairs={{0,4},{1,5},{2,6},{3,7},{4,0},{5,1},{6,2},{7,3},{8,12},{9,13},{10,... | collective-permute-start | bytes 6291464 | tf_op jit(solution)/shard_map/ppermute | solution.py:364
  4.8 2.1 fusion
  7.0 1.6 collective-permute-start.4
  8.6 1.5 collective-permute-start.3
  11.2 66.8 %collective-permute-done = f32[2,512]{1,0:T(2,128)S(1)} collective-permute-done((f32[2,512]{1,0:T(2,128)S(1)}, f32[2,512]{1,0:T(2,128)S(1)}, u32[]{:S(2)}, u32[]{:S(2)}) %collective-permute-start) | collective-permute-done | bytes 4128 | tf_op jit(solution)/shard_map/ppermute | solution.py:360
  78.4 42.0 %collective-permute-done.1 = f32[2,512]{1,0:T(2,128)S(1)} collective-permute-done((f32[2,512]{1,0:T(2,128)S(1)}, f32[2,512]{1,0:T(2,128)S(1)}, u32[]{:S(2)}, u32[]{:S(2)}) %collective-permute-start.1) | collective-permute-done | bytes 4128 | tf_op jit(solution)/shard_map/ppermute | solution.py:360
  121.0 4.0 %collective-permute-done.2 = f32[2,512]{1,0:T(2,128)S(1)} collective-permute-done((f32[2,512]{1,0:T(2,128)S(1)}, f32[2,512]{1,0:T(2,128)S(1)}, u32[]{:S(2)}, u32[]{:S(2)}) %collective-permute-start.2) | collective-permute-done | bytes 4128 | tf_op jit(solution)/shard_map/ppermute | solution.py:360
  125.0 2.6 collective-permute-start.6
  130.2 5.5 %collective-permute-start.9 = (f32[128,4096]{1,0:T(8,128)}, f32[128,4096]{1,0:T(8,128)}, u32[]{:S(2)}, u32[]{:S(2)}) collective-permute-start(f32[128,4096]{1,0:T(8,128)} %collective-permute-done.8.refs_8_.refs_7_), channel_id=1, source_target_pairs={{0,8},{8,16},{16,24},{1,9},{9,17},{17,25},{2,10},{10,18},{18,26},{... | collective-permute-start | bytes 6291464 | tf_op jit(solution)/shard_map/ppermute | solution.py:21
  135.7 1.5 collective-permute-start.11
  145.2 22.2 %density_rows.2 = (f32[6,1,384]{2,1,0:T(1,128)}, bf16[8,384,1024]{2,1,0:T(8,128)(2,1)}, bf16[8,384,1024]{2,1,0:T(8,128)(2,1)}) custom-call(s32[3]{0:T(128)} %pad_add_fusion.where, s32[64]{0:T(128)} %reshape.16.union, f32[2,384,1024]{2,1,0:T(8,128)} %refs_0_.1, f32[2,384,1024]{2,1,0:T(8,128)} %copy-done.2, f32[1,384,1024]{2,1,0:T(8,128)} %collective-permute-done.4.refs_2_, ...), custom_call_target="tpu_custom_call" | custom-call | flops 3623878656 | bytes 31457280 | tf_op jit(solution)/shard_map/density_rows/pallas_call | solution.py:244
  167.4 13.2 %collective-permute-done.12.refs_1_ = f32[1,256,1024]{2,1,0:T(8,128)} collective-permute-done((f32[1,256,1024]{2,1,0:T(8,128)}, f32[1,256,1024]{2,1,0:T(8,128)}, u32[]{:S(2)}, u32[]{:S(2)}) %collective-permute-start.12) | collective-permute-done | bytes 1048608 | tf_op jit(solution)/shard_map/ppermute | solution.py:360
  180.6 11.2 %density_rows.3 = (f32[2,1,384]{2,1,0:T(1,128)}, bf16[8,384,1024]{2,1,0:T(8,128)(2,1)}, bf16[8,384,1024]{2,1,0:T(8,128)(2,1)}) custom-call(s32[3]{0:T(128)} %pad_add_fusion.where, s32[64]{0:T(128)} %reshape.16.union, f32[1,384,1024]{2,1,0:T(8,128)} %collective-permute-done.11.refs_0_, ...), custom_call_target="tpu_custom_call", output_to_operand_aliasing={{1}: (11, {}), {2}: (12, {})} | custom-call | flops 1207959552 | bytes 18874368 | tf_op jit(solution)/shard_map/density_rows/pallas_call | solution.py:244
  192.7 2.4 collective-permute-start.15
  197.1 2.6 collective-permute-done.16
  200.3 4.1 %potential_net.1.scale_ref = f32[8,1,384]{2,1,0:T(1,128)} custom-call(f32[8,1,384]{2,1,0:T(1,128)} %reshape.18.rho_ref, f32[8,1,384]{2,1,0:T(1,128)} %reshape.19.weight_ref, f32[256,1]{1,0:T(8,128)} %copy.15.scale_ref, f32[256,1]{1,0:T(8,128)} %copy.16.shift_ref, f32[256,256]{1,0:T(8,128)} %bitcast.10, f32[256,1]{1,0:T(8,128)} %copy.17.bias_ref, ...), custom_call_target="tpu_custom_call" | custom-call | tf_op jit(solution)/shard_map/potential_net/pallas_call | solution.py:405
  204.4 11.3 %potential_rows.5 = (f32[128,1024]{1,0:T(8,128)}, f32[128,2048]{1,0:T(8,128)}, f32[128,1024]{1,0:T(8,128)}, f32[128,1024]{1,0:T(8,128)}, f32[128,2048]{1,0:T(8,128)}, /*index=5*/f32[128,1024]{1,0:T(8,128)}) custom-call(s32[3]{0:T(128)} %pad_add_fusion.where, s32[64]{0:T(128)} %reshape.16.union, bf16[8,384,1024]{2,1,0:T(8,128)(2,1)} %get-tuple-element.30.high_ref, ...), custom_call_target="tpu_custom_call" | custom-call | flops 3221225472 | bytes 16777216 | tf_op jit(solution)/shard_map/potential_rows/pallas_call | solution.py:280
  217.0 22.2 %collective-permute-start.21 = (f32[128,2048]{1,0:T(8,128)}, f32[128,2048]{1,0:T(8,128)S(1)}, u32[]{:S(2)}, u32[]{:S(2)}) collective-permute-start(f32[128,2048]{1,0:T(8,128)} %get-tuple-element.37), channel_id=1, source_target_pairs={{0,8},{8,16},{16,24},{1,9},{9,17},{17,25},{2,10},{10,18},{18,26},{... | collective-permute-start | bytes 3145736 | tf_op jit(solution)/shard_map/ppermute | solution.py:435
  239.2 12.6 %potential_rows.7 = (f32[128,1024]{1,0:T(8,128)}, f32[128,2048]{1,0:T(8,128)}, f32[128,1024]{1,0:T(8,128)}, f32[128,1024]{1,0:T(8,128)}, f32[128,2048]{1,0:T(8,128)}, /*index=5*/f32[128,1024]{1,0:T(8,128)}) custom-call(s32[3]{0:T(128)} %pad_add_fusion.where, s32[64]{0:T(128)} %reshape.16.union, bf16[8,384,1024]{2,1,0:T(8,128)(2,1)} %get-tuple-element.30.high_ref, ...), custom_call_target="tpu_custom_call" | custom-call | flops 3221225472 | bytes 16777216 | tf_op jit(solution)/shard_map/potential_rows/pallas_call | solution.py:280
  253.8 1.5 collective-permute-start.23
  255.3 9.9 %potential_rows.4 = (f32[128,1024]{1,0:T(8,128)}, f32[128,2048]{1,0:T(8,128)}, f32[128,1024]{1,0:T(8,128)}) custom-call(s32[3]{0:T(128)} %pad_add_fusion.where, s32[64]{0:T(128)} %reshape.16.union, bf16[8,384,1024]{2,1,0:T(8,128)(2,1)} %get-tuple-element.30.high_ref, bf16[8,384,1024]{2,1,0:T(8,128)(2,1)} %get-tuple-element.31.low_ref, ...), custom_call_target="tpu_custom_call" | custom-call | flops 1610612736 | bytes 14680064 | tf_op jit(solution)/shard_map/potential_rows/pallas_call | solution.py:280
  267.2 9.3 %collective-permute-start.18 = (f32[128,1024]{1,0:T(8,128)}, f32[128,1024]{1,0:T(8,128)S(1)}, u32[]{:S(2)}, u32[]{:S(2)}) collective-permute-start(f32[128,1024]{1,0:T(8,128)} %get-tuple-element.34), channel_id=1, source_target_pairs={{0,8},{8,16},{1,9},{9,17},{2,10},{10,18},{3,11},{11,19},{4,12},{12... | collective-permute-start | bytes 1572872 | tf_op jit(solution)/shard_map/ppermute | solution.py:435
  276.6 2.5 add_add_fusion
  280.6 7.2 %collective-permute-start.30 = (f32[128,2048]{1,0:T(8,128)}, f32[128,2048]{1,0:T(8,128)S(1)}, u32[]{:S(2)}, u32[]{:S(2)}) collective-permute-start(f32[128,2048]{1,0:T(8,128)} %get-tuple-element.48), channel_id=1, source_target_pairs={{0,8},{8,16},{16,24},{1,9},{9,17},{17,25},{2,10},{10,18},{18,26},{... | collective-permute-start | bytes 3145736 | tf_op jit(solution)/shard_map/ppermute | solution.py:435
  287.8 4.4 %collective-permute-start.29 = (f32[128,1024]{1,0:T(8,128)S(1)}, f32[128,1024]{1,0:T(8,128)}, u32[]{:S(2)}, u32[]{:S(2)}) collective-permute-start(f32[128,1024]{1,0:T(8,128)S(1)} %copy-done.19), channel_id=1, source_target_pairs={{0,8},{8,16},{1,9},{9,17},{2,10},{10,18},{3,11},{11,19},{4,12},{12... | collective-permute-start | bytes 1572872 | tf_op jit(solution)/shard_map/ppermute | solution.py:435
  292.2 1.5 collective-permute-start.31
  293.7 3.0 collective-permute-start.22
  296.7 2.0 add_add_fusion.1
  301.0 1.9 collective-permute-start.19
  302.9 11.4 %potential_rows.6 = (f32[128,1024]{1,0:T(8,128)}, f32[128,2048]{1,0:T(8,128)}, f32[128,1024]{1,0:T(8,128)}) custom-call(s32[3]{0:T(128)} %pad_add_fusion.where, s32[64]{0:T(128)} %reshape.16.union, bf16[8,384,1024]{2,1,0:T(8,128)(2,1)} %get-tuple-element.30.high_ref, bf16[8,384,1024]{2,1,0:T(8,128)(2,1)} %get-tuple-element.31.low_ref, ...), custom_call_target="tpu_custom_call" | custom-call | flops 1610612736 | bytes 14680064 | tf_op jit(solution)/shard_map/potential_rows/pallas_call | solution.py:280
  314.9 56.4 %collective-permute-done.19.refs_0_ = f32[128,1024]{1,0:T(8,128)} collective-permute-done((f32[128,1024]{1,0:T(8,128)}, f32[128,1024]{1,0:T(8,128)}, u32[]{:S(2)}, u32[]{:S(2)}) %collective-permute-start.19) | collective-permute-done | bytes 524320 | tf_op jit(solution)/shard_map/ppermute | solution.py:443
  373.0 5.2 %joined_rows.1 = f32[128,4096]{1,0:T(8,128)} custom-call(f32[128,1024]{1,0:T(8,128)} %collective-permute-done.19.refs_0_, f32[128,2048]{1,0:T(8,128)} %copy-done.5, f32[128,1024]{1,0:T(8,128)} %collective-permute-done.25.refs_2_, f32[128,1024]{1,0:T(8,128)} %get-tuple-element.41.refs_3_, f32[128,2048]{1,0:T(8,128)} %get-tuple-element.42.refs_4_, ...), custom_call_target="tpu_custom_call" | custom-call | flops 2097152 | bytes 10485760 | tf_op jit(solution)/shard_map/joined_rows/pallas_call | solution.py:314
  (103 shorter events, 27.4 us)
Async XLA Ops:
  0.7 128.2 %collective-permute-start.8 = (f32[128,4096]{1,0:T(8,128)}, f32[128,4096]{1,0:T(8,128)}, u32[]{:S(2)}, u32[]{:S(2)}) collective-permute-start(f32[128,4096]{1,0:T(8,128)} %refs_4_.1), channel_id=1, source_target_pairs={{0,4},{1,5},{2,6},{3,7},{4,0},{5,1},{6,2},{7,3},{8,12},{9,13},{10,... | collective-permute-start | bytes 6291464 | tf_op jit(solution)/shard_map/ppermute | solution.py:364
  7.0 120.6 %collective-permute-start.4 = (f32[1,384,1024]{2,1,0:T(8,128)S(1)}, f32[1,384,1024]{2,1,0:T(8,128)}, u32[]{:S(2)}, u32[]{:S(2)}) collective-permute-start(f32[1,384,1024]{2,1,0:T(8,128)S(1)} %get-tuple-element.51), channel_id=1, source_target_pairs={{0,2},{1,3},{2,0},{3,1},{4,6},{5,7},{6,4},{7,5},{8,10},{9,11},{10,... | collective-permute-start | bytes 4718600 | tf_op jit(solution)/shard_map/ppermute | solution.py:360
  8.6 129.7 %collective-permute-start.3 = (f32[2,384,1024]{2,1,0:T(8,128)S(1)}, f32[2,384,1024]{2,1,0:T(8,128)S(1)}, u32[]{:S(2)}, u32[]{:S(2)}) collective-permute-start(f32[2,384,1024]{2,1,0:T(8,128)S(1)} %copy-done), channel_id=1, source_target_pairs={{0,1},{1,0},{2,3},{3,2},{4,5},{5,4},{6,7},{7,6},{8,9},{9,8},{10,11... | collective-permute-start | bytes 9437192 | tf_op jit(solution)/shard_map/ppermute | solution.py:360
  10.1 120.1 %collective-permute-start.5 = (f32[1,384,1024]{2,1,0:T(8,128)S(1)}, f32[1,384,1024]{2,1,0:T(8,128)S(1)}, u32[]{:S(2)}, u32[]{:S(2)}) collective-permute-start(f32[1,384,1024]{2,1,0:T(8,128)S(1)} %get-tuple-element.50), channel_id=1, source_target_pairs={{0,2},{1,3},{2,0},{3,1},{4,6},{5,7},{6,4},{7,5},{8,10},{9,11},{10,... | collective-permute-start | bytes 4718600 | tf_op jit(solution)/shard_map/ppermute | solution.py:360
  10.6 67.4 %collective-permute-start = (f32[2,512]{1,0:T(2,128)S(1)}, f32[2,512]{1,0:T(2,128)S(1)}, u32[]{:S(2)}, u32[]{:S(2)}) collective-permute-start(f32[2,512]{1,0:T(2,128)S(1)} %select_maximum_fusion), channel_id=1, source_target_pairs={{0,1},{1,0},{2,3},{3,2},{4,5},{5,4},{6,7},{7,6},{8,9},{9,8},{10,11... | collective-permute-start | bytes 12296 | tf_op jit(solution)/shard_map/ppermute | solution.py:360
  78.0 42.5 %collective-permute-start.1 = (f32[2,512]{1,0:T(2,128)S(1)}, f32[2,512]{1,0:T(2,128)S(1)}, u32[]{:S(2)}, u32[]{:S(2)}) collective-permute-start(f32[2,512]{1,0:T(2,128)S(1)} %select_maximum_fusion), channel_id=1, source_target_pairs={{0,2},{1,3},{2,0},{3,1},{4,6},{5,7},{6,4},{7,5},{8,10},{9,11},{10,... | collective-permute-start | bytes 12296 | tf_op jit(solution)/shard_map/ppermute | solution.py:360
  120.5 4.5 %collective-permute-start.2 = (f32[2,512]{1,0:T(2,128)S(1)}, f32[2,512]{1,0:T(2,128)S(1)}, u32[]{:S(2)}, u32[]{:S(2)}) collective-permute-start(f32[2,512]{1,0:T(2,128)S(1)} %select_maximum_fusion), channel_id=1, source_target_pairs={{0,3},{1,2},{2,1},{3,0},{4,7},{5,6},{6,5},{7,4},{8,11},{9,10},{10,... | collective-permute-start | bytes 12296 | tf_op jit(solution)/shard_map/ppermute | solution.py:360
  125.0 10.7 %collective-permute-start.6 = (f32[128,4096]{1,0:T(8,128)}, f32[128,4096]{1,0:T(8,128)}, u32[]{:S(2)}, u32[]{:S(2)}) collective-permute-start(f32[128,4096]{1,0:T(8,128)} %refs_4_.1), channel_id=1, source_target_pairs={{0,8},{8,16},{16,24},{1,9},{9,17},{17,25},{2,10},{10,18},{18,26},{... | collective-permute-start | bytes 6291464 | tf_op jit(solution)/shard_map/ppermute | solution.py:21
  127.6 16.4 %collective-permute-start.7 = (f32[128,4096]{1,0:T(8,128)}, f32[128,4096]{1,0:T(8,128)}, u32[]{:S(2)}, u32[]{:S(2)}) collective-permute-start(f32[128,4096]{1,0:T(8,128)} %refs_4_.1), channel_id=1, source_target_pairs={{8,0},{16,8},{24,16},{9,1},{17,9},{25,17},{10,2},{18,10},{26,18},{... | collective-permute-start | bytes 6291464 | tf_op jit(solution)/shard_map/ppermute | solution.py:21
  128.9 16.3 %collective-permute-start.10 = (f32[128,4096]{1,0:T(8,128)}, f32[128,4096]{1,0:T(8,128)}, u32[]{:S(2)}, u32[]{:S(2)}) collective-permute-start(f32[128,4096]{1,0:T(8,128)} %collective-permute-done.8.refs_8_.refs_7_), channel_id=1, source_target_pairs={{8,0},{16,8},{24,16},{9,1},{17,9},{25,17},{10,2},{18,10},{26,18},{... | collective-permute-start | bytes 6291464 | tf_op jit(solution)/shard_map/ppermute | solution.py:21
  130.2 15.0 %collective-permute-start.9 = (f32[128,4096]{1,0:T(8,128)}, f32[128,4096]{1,0:T(8,128)}, u32[]{:S(2)}, u32[]{:S(2)}) collective-permute-start(f32[128,4096]{1,0:T(8,128)} %collective-permute-done.8.refs_8_.refs_7_), channel_id=1, source_target_pairs={{0,8},{8,16},{16,24},{1,9},{9,17},{17,25},{2,10},{10,18},{18,26},{... | collective-permute-start | bytes 6291464 | tf_op jit(solution)/shard_map/ppermute | solution.py:21
  135.7 44.9 %collective-permute-start.11 = (f32[1,384,1024]{2,1,0:T(8,128)}, f32[1,384,1024]{2,1,0:T(8,128)}, u32[]{:S(2)}, u32[]{:S(2)}) collective-permute-start(f32[1,384,1024]{2,1,0:T(8,128)} %collective-permute-done.4.refs_2_), channel_id=1, source_target_pairs={{0,1},{1,0},{2,3},{3,2},{4,5},{5,4},{6,7},{7,6},{8,9},{9,8},{10,11... | collective-permute-start | bytes 4718600 | tf_op jit(solution)/shard_map/ppermute | solution.py:360
  138.3 42.3 %collective-permute-start.12 = (f32[1,256,1024]{2,1,0:T(8,128)}, f32[1,256,1024]{2,1,0:T(8,128)}, u32[]{:S(2)}, u32[]{:S(2)}) collective-permute-start(f32[1,256,1024]{2,1,0:T(8,128)} %slice.28), channel_id=1, source_target_pairs={{0,1},{1,0},{2,3},{3,2},{4,5},{5,4},{6,7},{7,6},{8,9},{9,8},{10,11... | collective-permute-start | bytes 3145736 | tf_op jit(solution)/shard_map/ppermute | solution.py:360
  144.0 36.6 %collective-permute-start.13 = (f32[1,128,1024]{2,1,0:T(8,128)}, f32[1,128,1024]{2,1,0:T(8,128)}, u32[]{:S(2)}, u32[]{:S(2)}) collective-permute-start(f32[1,128,1024]{2,1,0:T(8,128)} %slice.29), channel_id=1, source_target_pairs={{0,2},{1,3},{2,0},{3,1},{4,6},{5,7},{6,4},{7,5},{8,10},{9,11},{10,... | collective-permute-start | bytes 1572872 | tf_op jit(solution)/shard_map/ppermute | solution.py:360
  192.6 4.5 %collective-permute-start.14 = (f32[2,2,2,384]{3,2,1,0:T(2,128)S(1)}, f32[2,2,2,384]{3,2,1,0:T(2,128)S(1)}, u32[]{:S(2)}, u32[]{:S(2)}) collective-permute-start(f32[2,2,2,384]{3,2,1,0:T(2,128)S(1)} %reshape.17), channel_id=1, source_target_pairs={{0,1},{1,0},{2,3},{3,2},{4,5},{5,4},{6,7},{7,6},{8,9},{9,8},{10,11... | collective-permute-start | bytes 36872 | tf_op jit(solution)/shard_map/ppermute | solution.py:360
  192.7 4.4 %collective-permute-start.15 = (f32[2,2,2,384]{3,2,1,0:T(2,128)S(1)}, f32[2,2,2,384]{3,2,1,0:T(2,128)S(1)}, u32[]{:S(2)}, u32[]{:S(2)}) collective-permute-start(f32[2,2,2,384]{3,2,1,0:T(2,128)S(1)} %reshape.17), channel_id=1, source_target_pairs={{0,2},{1,3},{2,0},{3,1},{4,6},{5,7},{6,4},{7,5},{8,10},{9,11},{10,... | collective-permute-start | bytes 36872 | tf_op jit(solution)/shard_map/ppermute | solution.py:360
  195.0 4.6 %collective-permute-start.16 = (f32[2,2,2,384]{3,2,1,0:T(2,128)S(1)}, f32[2,2,2,384]{3,2,1,0:T(2,128)S(1)}, u32[]{:S(2)}, u32[]{:S(2)}) collective-permute-start(f32[2,2,2,384]{3,2,1,0:T(2,128)S(1)} %reshape.17), channel_id=1, source_target_pairs={{0,3},{1,2},{2,1},{3,0},{4,7},{5,6},{6,5},{7,4},{8,11},{9,10},{10,... | collective-permute-start | bytes 36872 | tf_op jit(solution)/shard_map/ppermute | solution.py:360
  215.7 50.2 %collective-permute-start.20 = (f32[128,2048]{1,0:T(8,128)}, f32[128,2048]{1,0:T(8,128)S(1)}, u32[]{:S(2)}, u32[]{:S(2)}) collective-permute-start(f32[128,2048]{1,0:T(8,128)} %get-tuple-element.36), channel_id=1, source_target_pairs={{8,0},{16,8},{24,16},{9,1},{17,9},{25,17},{10,2},{18,10},{26,18},{... | collective-permute-start | bytes 3145736 | tf_op jit(solution)/shard_map/ppermute | solution.py:435
  217.0 50.2 %collective-permute-start.21 = (f32[128,2048]{1,0:T(8,128)}, f32[128,2048]{1,0:T(8,128)S(1)}, u32[]{:S(2)}, u32[]{:S(2)}) collective-permute-start(f32[128,2048]{1,0:T(8,128)} %get-tuple-element.37), channel_id=1, source_target_pairs={{0,8},{8,16},{16,24},{1,9},{9,17},{17,25},{2,10},{10,18},{18,26},{... | collective-permute-start | bytes 3145736 | tf_op jit(solution)/shard_map/ppermute | solution.py:435
  251.8 13.4 %collective-permute-start.26 = (f32[128,1024]{1,0:T(8,128)}, f32[128,1024]{1,0:T(8,128)S(1)}, u32[]{:S(2)}, u32[]{:S(2)}) collective-permute-start(f32[128,1024]{1,0:T(8,128)} %get-tuple-element.44), channel_id=1, source_target_pairs={{8,0},{9,1},{10,2},{11,3},{12,4},{13,5},{14,6},{15,7}} | collective-permute-start | bytes 1572872 | tf_op jit(solution)/shard_map/ppermute | solution.py:435
  253.1 26.0 %collective-permute-start.28 = (f32[128,1024]{1,0:T(8,128)}, f32[128,1024]{1,0:T(8,128)S(1)}, u32[]{:S(2)}, u32[]{:S(2)}) collective-permute-start(f32[128,1024]{1,0:T(8,128)} %get-tuple-element.46), channel_id=1, source_target_pairs={{16,8},{24,16},{17,9},{25,17},{18,10},{26,18},{19,11},{27,19},{20,... | collective-permute-start | bytes 1572872 | tf_op jit(solution)/shard_map/ppermute | solution.py:435
  253.8 26.7 %collective-permute-start.23 = (f32[128,1024]{1,0:T(8,128)}, f32[128,1024]{1,0:T(8,128)}, u32[]{:S(2)}, u32[]{:S(2)}) collective-permute-start(f32[128,1024]{1,0:T(8,128)} %get-tuple-element.39), channel_id=1, source_target_pairs={{16,8},{24,16},{17,9},{25,17},{18,10},{26,18},{19,11},{27,19},{20,... | collective-permute-start | bytes 1572872 | tf_op jit(solution)/shard_map/ppermute | solution.py:435
  265.2 22.6 %collective-permute-start.24 = (f32[128,1024]{1,0:T(8,128)}, f32[128,1024]{1,0:T(8,128)S(1)}, u32[]{:S(2)}, u32[]{:S(2)}) collective-permute-start(f32[128,1024]{1,0:T(8,128)} %get-tuple-element.40), channel_id=1, source_target_pairs={{16,24},{17,25},{18,26},{19,27},{20,28},{21,29},{22,30},{23,31}} | collective-permute-start | bytes 1572872 | tf_op jit(solution)/shard_map/ppermute | solution.py:435
  265.9 26.3 %collective-permute-start.17 = (f32[128,1024]{1,0:T(8,128)}, f32[128,1024]{1,0:T(8,128)S(1)}, u32[]{:S(2)}, u32[]{:S(2)}) collective-permute-start(f32[128,1024]{1,0:T(8,128)} %get-tuple-element.33), channel_id=1, source_target_pairs={{8,0},{9,1},{10,2},{11,3},{12,4},{13,5},{14,6},{15,7}} | collective-permute-start | bytes 1572872 | tf_op jit(solution)/shard_map/ppermute | solution.py:435
  267.2 26.4 %collective-permute-start.18 = (f32[128,1024]{1,0:T(8,128)}, f32[128,1024]{1,0:T(8,128)S(1)}, u32[]{:S(2)}, u32[]{:S(2)}) collective-permute-start(f32[128,1024]{1,0:T(8,128)} %get-tuple-element.34), channel_id=1, source_target_pairs={{0,8},{8,16},{1,9},{9,17},{2,10},{10,18},{3,11},{11,19},{4,12},{12... | collective-permute-start | bytes 1572872 | tf_op jit(solution)/shard_map/ppermute | solution.py:435
  279.1 92.3 %collective-permute-start.27 = (f32[128,2048]{1,0:T(8,128)}, f32[128,2048]{1,0:T(8,128)S(1)}, u32[]{:S(2)}, u32[]{:S(2)}) collective-permute-start(f32[128,2048]{1,0:T(8,128)} %get-tuple-element.45), channel_id=1, source_target_pairs={{8,0},{16,8},{24,16},{9,1},{17,9},{25,17},{10,2},{18,10},{26,18},{... | collective-permute-start | bytes 3145736 | tf_op jit(solution)/shard_map/ppermute | solution.py:435
  280.6 90.8 %collective-permute-start.30 = (f32[128,2048]{1,0:T(8,128)}, f32[128,2048]{1,0:T(8,128)S(1)}, u32[]{:S(2)}, u32[]{:S(2)}) collective-permute-start(f32[128,2048]{1,0:T(8,128)} %get-tuple-element.48), channel_id=1, source_target_pairs={{0,8},{8,16},{16,24},{1,9},{9,17},{17,25},{2,10},{10,18},{18,26},{... | collective-permute-start | bytes 3145736 | tf_op jit(solution)/shard_map/ppermute | solution.py:435
  287.8 11.8 %collective-permute-start.29 = (f32[128,1024]{1,0:T(8,128)S(1)}, f32[128,1024]{1,0:T(8,128)}, u32[]{:S(2)}, u32[]{:S(2)}) collective-permute-start(f32[128,1024]{1,0:T(8,128)S(1)} %copy-done.19), channel_id=1, source_target_pairs={{0,8},{8,16},{1,9},{9,17},{2,10},{10,18},{3,11},{11,19},{4,12},{12... | collective-permute-start | bytes 1572872 | tf_op jit(solution)/shard_map/ppermute | solution.py:435
  292.2 8.8 %collective-permute-start.31 = (f32[128,1024]{1,0:T(8,128)S(1)}, f32[128,1024]{1,0:T(8,128)}, u32[]{:S(2)}, u32[]{:S(2)}) collective-permute-start(f32[128,1024]{1,0:T(8,128)S(1)} %copy-done.18), channel_id=1, source_target_pairs={{16,24},{17,25},{18,26},{19,27},{20,28},{21,29},{22,30},{23,31}} | collective-permute-start | bytes 1572872 | tf_op jit(solution)/shard_map/ppermute | solution.py:435
  293.7 77.7 %collective-permute-start.22 = (f32[128,2048]{1,0:T(8,128)}, f32[128,2048]{1,0:T(8,128)S(1)}, u32[]{:S(2)}, u32[]{:S(2)}) collective-permute-start(f32[128,2048]{1,0:T(8,128)} %add_add_fusion), channel_id=1, source_target_pairs={{0,4},{1,5},{2,6},{3,7},{4,0},{5,1},{6,2},{7,3},{8,12},{9,13},{10,... | collective-permute-start | bytes 3145736 | tf_op jit(solution)/shard_map/ppermute | solution.py:443
  299.6 15.4 %collective-permute-start.25 = (f32[128,1024]{1,0:T(8,128)}, f32[128,1024]{1,0:T(8,128)}, u32[]{:S(2)}, u32[]{:S(2)}) collective-permute-start(f32[128,1024]{1,0:T(8,128)} %add_add_fusion.1), channel_id=1, source_target_pairs={{8,12},{9,13},{10,14},{11,15},{12,8},{13,9},{14,10},{15,11},{16,20... | collective-permute-start | bytes 1572872 | tf_op jit(solution)/shard_map/ppermute | solution.py:443
  301.0 70.3 %collective-permute-start.19 = (f32[128,1024]{1,0:T(8,128)}, f32[128,1024]{1,0:T(8,128)}, u32[]{:S(2)}, u32[]{:S(2)}) collective-permute-start(f32[128,1024]{1,0:T(8,128)} %add_add_fusion.2), channel_id=1, source_target_pairs={{0,4},{1,5},{2,6},{3,7},{4,0},{5,1},{6,2},{7,3},{8,12},{9,13},{10,... | collective-permute-start | bytes 1572872 | tf_op jit(solution)/shard_map/ppermute | solution.py:443
  (20 other events, 822.0 us)

commit v2 on v1

v2 whole, which is shorter than its diff:
```python
import functools
import math

import jax
import jax.numpy as jnp
from jax import lax
from jax.experimental import pallas as pl
from jax.experimental.pallas import tpu as pltpu

from jax.sharding import PartitionSpec as P

TILE = 128
U = 8
SPACE, DEV = "space", "dev"


highest = lax.Precision.HIGHEST


def passed_along(block, axis, distance):
    devices = range(lax.axis_size(axis))
    route = [(i - distance, i) for i in devices if i - distance in devices]
    return lax.ppermute(block, axis, route)


def potential_net(point_rho, in_scale, in_shift, hidden_weight, hidden_bias, out_weight):
    first_layer = jnp.tanh(point_rho[:, None] * in_scale[None, :] + in_shift[None, :])
    pre_act = (
        jnp.dot(first_layer, hidden_weight, precision=highest, preferred_element_type=jnp.float32)
        + hidden_bias[None, :]
    )
    second = jax.nn.silu(pre_act)
    return jnp.dot(second, out_weight, precision=highest, preferred_element_type=jnp.float32)


def place_columns(piece_block, centre, region, orbitals):
    canvas = jnp.zeros((piece_block.shape[0], orbitals + 2 * region), jnp.float32)
    canvas = lax.dynamic_update_slice_in_dim(canvas, piece_block, centre * region, 1)
    return canvas[:, region : region + orbitals]


def by_window(
    density_matrix,
    basis,
    union,
    weights,
    in_scale,
    in_shift,
    hidden_weight,
    hidden_bias,
    out_weight,
):
    _, orbitals = density_matrix.shape
    space_count = lax.axis_size(SPACE)
    region = orbitals // space_count
    window_cols = 3 * region
    region_tiles = region // TILE
    group_index = lax.axis_index(SPACE)
    padded = jnp.pad(density_matrix, ((0, 0), (region, region)))
    own_rows = lax.dynamic_slice_in_dim(padded, group_index * region, window_cols, 1)
    upward = lax.dynamic_slice_in_dim(padded, (group_index + 1) * region, window_cols, 1)
    downward = lax.dynamic_slice_in_dim(padded, (group_index - 1) * region, window_cols, 1)
    from_below = passed_along(upward, SPACE, 1)
    from_above = passed_along(downward, SPACE, -1)
    stacked = jnp.stack([from_below, own_rows, from_above])
    window = lax.all_gather(stacked, DEV, axis=1, tiled=True)
    blocks = window.reshape(3 * region_tiles, TILE, 3 * region_tiles, TILE)
    first_tile = (group_index - 1) * region_tiles
    partial_value = jnp.zeros_like(blocks)
    densities = []
    for batch_index in range(basis.shape[0]):
        values = basis[batch_index]
        union_width = values.shape[1]
        chosen = union[batch_index] - first_tile
        sub_block = blocks[chosen[:, None], :, chosen[None, :], :]
        sub_block = sub_block.transpose(0, 2, 1, 3).reshape(union_width, union_width)
        projected = jnp.dot(
            values, sub_block, precision=highest, preferred_element_type=jnp.float32
        )
        point_rho = jnp.sum(projected * values, axis=1)
        point_pot = potential_net(
            point_rho, in_scale, in_shift, hidden_weight, hidden_bias, out_weight
        )
        scaled = values * (weights[batch_index] * point_pot)[:, None]
        product = lax.dot_general(
            scaled,
            values,
            (((0,), (0,)), ((), ())),
            precision=highest,
            preferred_element_type=jnp.float32,
        )
        term_tile = product.reshape(U, TILE, U, TILE).transpose(0, 2, 1, 3)
        partial_value = partial_value.at[chosen[:, None], :, chosen[None, :], :].add(term_tile)
        densities.append(point_rho)
    density = jnp.stack(densities)
    partial_value = partial_value.reshape(3, region, window_cols)
    down_block = passed_along(partial_value[0], SPACE, -1)
    up_block = passed_along(partial_value[2], SPACE, 1)
    full_rows = place_columns(partial_value[1], group_index, region, orbitals)
    full_rows = full_rows + place_columns(down_block, group_index + 1, region, orbitals)
    full_rows = full_rows + place_columns(up_block, group_index - 1, region, orbitals)
    potential = lax.psum_scatter(full_rows, DEV, scatter_dimension=0, tiled=True)
    return (density, potential)


QUAD = 4
NT = (((1,), (1,)), ((), ()))
NN = (((1,), (0,)), ((), ()))


def split(value):
    high = value.astype(jnp.bfloat16)
    return high, (value - high.astype(jnp.float32)).astype(jnp.bfloat16)


def product(a, b, dims):
    return lax.dot_general(a, b, dims, preferred_element_type=jnp.float32)


def tile_at(index):
    return pl.ds(pl.multiple_of(index * TILE, TILE), TILE)


def place_of(tile, where, region_tiles):
    quads = region_tiles // QUAD
    mine = tile % QUAD == where[1]
    turn = (tile % region_tiles // QUAD - where[2] + quads) % quads
    return mine, turn, tile // region_tiles - where[0] + 1


def density_kernel(pieces, first, turns, row_cuts, region_tiles, where, union, *refs):
    n_x, n_rows = len(pieces), len(row_cuts)
    x_refs, row_refs = refs[:n_x], refs[n_x : n_x + n_rows]
    rho_ref, high_ref, low_ref, x_full, d_both, total, tiles, tile_sems = refs[-8:]
    step, steps = pl.program_id(0), pl.num_programs(0)

    def each_row(at, body):
        @pl.loop(0, U)
        def _(i):
            mine, turn, place = place_of(union[(first + at) * U + i], where, region_tiles)
            wanted = functools.reduce(jnp.logical_or, [turn == k for k in turns])

            @pl.when(mine & wanted)
            def _():
                body(i, (turn - turns[0]) * 3 + place)

    def fetch(at, slot):
        def fetch_row(i, row):
            for n in range(3 * len(turns)):

                @pl.when(row == n)
                def _():
                    @pl.loop(0, U)
                    def _(j):
                        column = union[(first + at) * U + j] * TILE
                        for row_ref, (of_row, start, end) in zip(row_refs, row_cuts, strict=True):
                            if of_row == n:

                                @pl.when((column >= start) & (column < end))
                                def _():
                                    here = pl.ds(pl.multiple_of(column - start, TILE), TILE)
                                    pltpu.make_async_copy(
                                        row_ref.at[:, here],
                                        tiles.at[slot, i, :, tile_at(j)],
                                        tile_sems.at[slot, i],
                                    ).start()

        each_row(at, fetch_row)

    slot = lax.rem(step, 2)

    @pl.when(step == 0)
    def _():
        fetch(step, slot)

    @pl.when(step + 1 < steps)
    def _():
        fetch(step + 1, 1 - slot)

    for x_ref, (start, count, point) in zip(x_refs, pieces, strict=True):

        @pl.when((step >= start) & (step < start + count))
        def _():
            value = x_ref[0]
            at = pl.ds(point, x_ref.shape[1])
            x_full[at, :] = value
            high_ref[0, at, :], low_ref[0, at, :] = split(value)

    total[...] = jnp.zeros_like(total)

    def add_row(i, row):
        block = tiles.at[slot, i]
        pltpu.make_async_copy(block, block, tile_sems.at[slot, i]).wait()
        d_both[:TILE], d_both[TILE:] = split(block[...])
        both = product(high_ref[0], d_both[...], NT)
        sums = both[:, :TILE] + (both[:, TILE:] + product(low_ref[0], d_both[:TILE], NT))
        total[...] += sums * x_full[:, tile_at(i)]

    each_row(step, add_row)
    ones = jnp.ones((8, TILE), jnp.float32)
    rho_ref[0] = lax.dot_general(
        ones, total[...], NT, precision=highest, preferred_element_type=jnp.float32
    )[:1]


def potential_kernel(counts, k, places, chunks, region_tiles, where, union, *refs):
    n_halves = 2 * len(counts)
    half_refs, scale_ref, out_refs = refs[:n_halves], refs[n_halves], refs[n_halves + 1 : -5]
    sums, term, highs, lows, sems = refs[-5:]
    copies = []
    for n, half_ref in enumerate(half_refs):
        at = pl.ds(sum(counts[: n // 2]), counts[n // 2])
        held = (highs, lows)[n % 2].at[at]
        copies.append(pltpu.make_async_copy(half_ref, held, sems.at[n]))
        copies[-1].start()
    sums[...] = jnp.zeros_like(sums)

    def add_row(batch, i, slot):
        here = tile_at(i)
        value = highs[batch, :, here].astype(jnp.float32)
        value = value + lows[batch, :, here].astype(jnp.float32)
        high, low = split(value.T * scale_ref[batch])
        both = product(jnp.concatenate([high, low]), highs[batch], NN)
        term[...] = both[:TILE] + (both[TILE:] + product(high, lows[batch], NN))
        for j in range(U):
            at = tile_at(union[batch * U + j])
            sums[slot, :, at] += term[:, j * TILE : (j + 1) * TILE]

    for n, count in enumerate(counts):
        for copy in copies[2 * n : 2 * n + 2]:
            copy.wait()

        @pl.loop(sum(counts[:n]) * U, sum(counts[: n + 1]) * U)
        def _(at):
            batch, i = at // U, at % U
            mine, turn, place = place_of(union[batch * U + i], where, region_tiles)
            wanted = functools.reduce(jnp.logical_or, [place == r for r in places])

            @pl.when(mine & (turn == k) & wanted)
            def _():
                slot = sum((place == r) * m for m, r in enumerate(places))
                add_row(batch, i, slot)

    for n in range(len(places)):
        for c, (first, last) in enumerate(chunks):
            out_refs[n * len(chunks) + c][...] = sums[n, :, first:last]


def joined_kernel(chunks, *refs):
    out_ref, refs = refs[-1], refs[:-1]
    terms = len(refs) // len(chunks)
    for c, (first, last) in enumerate(chunks):
        value = refs[c][...]
        for n in range(1, terms):
            value = value + refs[n * len(chunks) + c][...]
        out_ref[:, first:last] = value


def added_kernel(sum_ref, term_ref, out_ref):
    out_ref[...] = sum_ref[...] + term_ref[...]


def net_kernel(rho_ref, weight_ref, hidden_ref, columns_ref, out_ref):
    scale, shift, bias, out_w = (columns_ref[:, n : n + 1] for n in range(4))
    h_high, h_low = split(hidden_ref[...])
    for b in range(rho_ref.shape[0]):
        first_layer = jnp.tanh(rho_ref[b] * scale + shift)
        f_high, f_low = split(first_layer)
        pre_act = (
            product(h_high, f_high, NN)
            + (product(h_high, f_low, NN) + product(h_low, f_high, NN))
            + bias
        )
        second = pre_act / (1.0 + jnp.exp(-pre_act))
        out_ref[b] = jnp.sum(out_w * second, axis=0, keepdims=True) * weight_ref[b]


def call_density(
    xs, pieces, rows, turns, where, union, region_tiles, first, points, keep=True
):
    width = xs[0].shape[2]
    steps = max(start + count for start, count, _ in pieces)

    def x_spec(x, start, count):
        return pl.BlockSpec(
            (1, *x.shape[1:]), lambda g, *_: (jnp.clip(g - start, 0, count - 1), 0, 0)
        )

    used = [(n, *piece) for n, row in enumerate(rows) for piece in row]
    row_cuts = [(n, start, start + block.shape[1]) for n, block, start in used]
    orbitals = max(end for _, _, end in row_cuts)
    halves = jax.ShapeDtypeStruct((steps, points, width), jnp.bfloat16)
    half_spec = pl.BlockSpec((1, points, width), lambda g, *_: (g, 0, 0))
    half_scratch = pltpu.VMEM((1, points, width), jnp.bfloat16)
    return pl.pallas_call(
        functools.partial(density_kernel, pieces, first, turns, row_cuts, region_tiles),
        out_shape=[jax.ShapeDtypeStruct((steps, 1, points), jnp.float32)] + [halves] * (2 * keep),
        grid_spec=pltpu.PrefetchScalarGridSpec(
            num_scalar_prefetch=2,
            grid=(steps,),
            in_specs=[
                x_spec(x, start, count) for x, (start, count, _) in zip(xs, pieces, strict=True)
            ]
            + [pl.BlockSpec(memory_space=pltpu.HBM)] * len(used),
            out_specs=[pl.BlockSpec((1, 1, points), lambda g, *_: (g, 0, 0))]
            + [half_spec] * (2 * keep),
            scratch_shapes=[half_scratch] * (2 - 2 * keep)
            + [
                pltpu.VMEM((points, width), jnp.float32),
                pltpu.VMEM((2 * TILE, width), jnp.bfloat16),
                pltpu.VMEM((points, TILE), jnp.float32),
                pltpu.VMEM((2, U, TILE, width), jnp.float32),
                pltpu.SemaphoreType.DMA((2, U)),
            ],
        ),
        cost_estimate=pl.CostEstimate(
            flops=3 * len(turns) * steps * points * width * width // QUAD,
            bytes_accessed=8 * steps * points * width + 4 * len(rows) * TILE * orbitals,
            transcendentals=0,
        ),
        name="density_rows",
    )(where, union, *xs, *[block for _, block, _ in used])


def call_potential(halves, scale, k, places, chunks, where, union, region_tiles):
    points, width = halves[0].shape[1:]
    counts = tuple(high.shape[0] for high in halves[::2])
    widths = [last - first for first, last in chunks] * len(places)
    in_vmem = pl.BlockSpec(memory_space=pltpu.VMEM)
    return pl.pallas_call(
        functools.partial(potential_kernel, counts, k, places, chunks, region_tiles),
        out_shape=[jax.ShapeDtypeStruct((TILE, w), jnp.float32) for w in widths],
        in_specs=[pl.BlockSpec(memory_space=pltpu.SMEM)] * 2
        + [pl.BlockSpec(memory_space=pltpu.HBM)] * len(halves)
        + [in_vmem],
        out_specs=[in_vmem] * len(widths),
        scratch_shapes=[
            pltpu.VMEM((len(places), TILE, chunks[-1][1]), jnp.float32),
            pltpu.VMEM((TILE, width), jnp.float32),
            pltpu.VMEM((sum(counts), points, width), jnp.bfloat16),
            pltpu.VMEM((sum(counts), points, width), jnp.bfloat16),
            pltpu.SemaphoreType.DMA((len(halves),)),
        ],
        cost_estimate=pl.CostEstimate(
            flops=2 * len(places) * sum(counts) * points * width * width // QUAD,
            bytes_accessed=4 * sum(counts) * points * width
            + 4 * len(places) * TILE * chunks[-1][1],
            transcendentals=0,
        ),
        name="potential_rows",
    )(where, union, *halves, scale)


def call_joined(terms, chunks):
    rows = 4
    height = TILE // rows
    widths = [last - first for first, last in chunks]
    flat = [block for term in terms for block in term]
    return pl.pallas_call(
        functools.partial(joined_kernel, chunks),
        out_shape=jax.ShapeDtypeStruct((TILE, chunks[-1][1]), jnp.float32),
        grid=(rows,),
        in_specs=[pl.BlockSpec((height, w), lambda g: (g, 0)) for w in widths] * len(terms),
        out_specs=pl.BlockSpec((height, chunks[-1][1]), lambda g: (g, 0)),
        cost_estimate=pl.CostEstimate(
            flops=TILE * chunks[-1][1] * len(terms),
            bytes_accessed=4 * TILE * chunks[-1][1] * (len(terms) + 1),
            transcendentals=0,
        ),
        compiler_params=pltpu.CompilerParams(vmem_limit_bytes=20 * 2**20),
        name="joined_rows",
    )(*flat)


def call_added(total, term, first):
    height, width = term.shape
    cut = math.gcd(first, width)
    spec = pl.BlockSpec((height, cut), lambda g: (0, first // cut + g))
    return pl.pallas_call(
        added_kernel,
        out_shape=jax.ShapeDtypeStruct(total.shape, jnp.float32),
        grid=(width // cut,),
        in_specs=[spec, pl.BlockSpec((height, cut), lambda g: (0, g))],
        out_specs=spec,
        input_output_aliases={0: 0},
        cost_estimate=pl.CostEstimate(
            flops=term.size, bytes_accessed=12 * term.size, transcendentals=0
        ),
        compiler_params=pltpu.CompilerParams(vmem_limit_bytes=20 * 2**20),
        name="added_rows",
    )(total, term)


def column_groups(regions):
    meets = [tuple(r for r in range(regions) if abs(r - c) <= 2) for c in range(regions)]
    groups = []
    for c in range(regions):
        if groups and meets[c] == groups[-1][2]:
            groups[-1] = (groups[-1][0], c + 1, meets[c])
        else:
            groups.append((c, c + 1, meets[c]))
    return groups


def by_quads(
    density_matrix,
    basis,
    union,
    weights,
    in_scale,
    in_shift,
    hidden_weight,
    hidden_bias,
    out_weight,
):
    orbitals = density_matrix.shape[1]
    batches, points, _ = basis.shape
    n_dev = lax.axis_size(DEV)
    region_tiles = orbitals // lax.axis_size(SPACE) // TILE
    quads = n_dev // QUAD
    space_index, dev_index = lax.axis_index(SPACE), lax.axis_index(DEV)
    where = jnp.stack([space_index, dev_index % QUAD, dev_index // QUAD])

    def swapped(block, flip):
        return lax.ppermute(block, DEV, [(d, d ^ flip) for d in range(n_dev)])

    def to_space(block, distance):
        return passed_along(block, SPACE, distance)

    regions = lax.axis_size(SPACE)
    groups = column_groups(regions)
    chunks = tuple((c * orbitals // regions, end * orbitals // regions) for c, end, _ in groups)
    order = sorted(range(len(groups)), key=lambda n: groups[n][0] - groups[n][1])

    def piece_to_space(block, n, distance, window_of_sender):
        first, last, _ = groups[n]
        route = [
            (r, r + distance)
            for r in range(regions)
            if 0 <= r + distance < regions
            and first - 1 <= r + distance * (not window_of_sender) <= last
        ]
        return lax.ppermute(block, SPACE, route)

    def piece_turned(block, n, k):
        route = [
            (r * n_dev + d, r * n_dev + (d + QUAD * k) % n_dev)
            for r in groups[n][2]
            for d in range(n_dev)
        ]
        return lax.ppermute(block, (SPACE, DEV), route)

    beside = swapped(basis, 1)
    rows = [
        [(to_space(density_matrix, 1), 0)],
        [(density_matrix, 0)],
        [(to_space(density_matrix, -1), 0)],
    ]
    for k in range(1, quads):
        base = [
            piece_turned(density_matrix[:, start:end], n, -k)
            for n, (start, end) in enumerate(chunks)
        ]
        for distance in (1, 0, -1):
            pieces = base
            if distance:
                pieces = [piece_to_space(base[n], n, distance, False) for n in range(len(chunks))]
            rows.append([(block, start) for block, (start, _) in zip(pieces, chunks, strict=True)])
    last, middle = batches - 1, 2 * points // 3 // 16 * 16
    cuts = ((0, middle), (middle, points))
    across = [swapped(basis[b : b + 1], 2) for b in range(last)]
    across.append([swapped(basis[last:, p:end], 2) for p, end in cuts])
    corner = [swapped(across[b], 1) for b in range(last)]
    corner.append([swapped(across[last][0], 1), swapped(beside[last:, middle:], 2)])

    small = jnp.concatenate([weights, union.astype(jnp.float32)], axis=1)
    small = jnp.pad(small, ((0, 0), (0, -small.shape[1] % TILE)))
    small = [small] + [swapped(small, flip) for flip in range(1, QUAD)]
    small = jnp.concatenate(small)
    all_weights = small[:, :points].reshape(-1, 1, points)
    tiles = small[:, points : points + U].astype(jnp.int32).reshape(-1)

    turns = tuple(range(quads))

    def density_of(blocks, turns, first, tiles=tiles, **options):
        xs, pieces, at = [], [], 0
        for block in blocks:
            if isinstance(block, list):
                xs += block
                pieces += [(at, 1, p) for p, _ in cuts]
                at += 1
            else:
                xs.append(block)
                pieces.append((at, block.shape[0], 0))
                at += block.shape[0]
        used = [row for k in turns for row in rows[3 * k : 3 * k + 3]]
        return call_density(
            xs, pieces, used, turns, where, tiles, region_tiles, first, points, **options
        )

    near = [beside, *across[:last]]
    rho_own, *own_halves = density_of([basis], turns[:1], 0, tiles=union.reshape(-1))
    rho_near, *near_halves = density_of(near, turns[:1], batches)
    rho_early = jnp.concatenate([rho_own, rho_near])
    if quads > 1:
        early = [basis, *near]
        rho_early = rho_early + density_of(early, turns[1:], 0, keep=False)[0]
    n_early = rho_early.shape[0]
    rho_late, *late_halves = density_of([across[last], *corner[:last]], turns, n_early)
    rho_last, *last_halves = density_of([corner[last]], turns, QUAD * batches - 1)
    halves = [*own_halves, *near_halves, *late_halves, *last_halves]
    part = jnp.concatenate([rho_early, rho_late, rho_last]).reshape(2, 2, batches, points)
    rho = (part + swapped(part, 1)[:, ::-1]) + (
        swapped(part, 2)[::-1] + swapped(part, 3)[::-1, ::-1]
    )
    density = rho[0, 0]

    scale = pl.pallas_call(
        net_kernel,
        out_shape=jax.ShapeDtypeStruct(all_weights.shape, jnp.float32),
        compiler_params=pltpu.CompilerParams(vmem_limit_bytes=20 * 2**20),
        name="potential_net",
    )(
        rho.reshape(-1, 1, points),
        all_weights,
        hidden_weight.T,
        jnp.stack([in_scale, in_shift, hidden_bias, out_weight], axis=1),
    )

    def part_rows(k, places):
        parts = call_potential(halves, scale, k, places, chunks, where, tiles, region_tiles)
        return [parts[n : n + len(chunks)] for n in range(0, len(parts), len(chunks))]

    moved = []
    for k in [*range(1, quads), 0]:
        below, above = part_rows(k, (0, 2))
        received = [None] * len(chunks)
        for n in order:
            received[n] = (
                piece_to_space(below[n], n, -1, True), piece_to_space(above[n], n, 1, True)
            )
        (inner,) = part_rows(k, (1,))
        if k:
            for n in order:
                block = inner[n] + received[n][0] + received[n][1]
                moved.append((piece_turned(block, n, k), chunks[n][0]))
        else:
            terms = [inner, [pair[0] for pair in received], [pair[1] for pair in received]]
    potential = call_joined(terms, chunks)
    for block, first in moved:
        potential = call_added(potential, block, first)
    return (density, potential)


def solution(mesh):
    in_specs = (
        P((SPACE, DEV), None),
        P((SPACE, DEV), None, None),
        P((SPACE, DEV), None),
        P((SPACE, DEV), None),
        P(),
        P(),
        P(),
        P(),
        P(),
    )
    out_specs = (P((SPACE, DEV), None), P((SPACE, DEV), None))
    devices = mesh.shape[SPACE] * mesh.shape[DEV]

    def whole_tile(density_matrix):
        return density_matrix.shape[0] == devices * TILE and mesh.shape[DEV] % QUAD == 0

    def mapped(plan):
        return jax.shard_map(
            plan, mesh=mesh, in_specs=in_specs, out_specs=out_specs, check_vma=False
        )

    def step(density_matrix, basis, *others):
        if not whole_tile(density_matrix):
            return mapped(by_window)(density_matrix, basis, *others)

        return mapped(by_quads)(
            density_matrix, basis, *others
        )

    return step
```

time: 383 us -> 370 us (0.966)
  starting transfers between devices: 85 us -> 69.6 us
  local copies, waits for them, and re-layouts: 12.4 us -> 21.5 us
  waiting for transfers between devices: 185 us -> 177 us
    unnamed x41 -> x81, local copies, waits for them, and re-layouts: 2.83 us -> 14.7 us
    ppermute x28 -> x37, waiting for transfers between devices: 185 us -> 177 us  [the longest x13 108 us: swapped(): return lax.ppermute(block, DEV, [(d, d ^ flip) for d in range(n_dev)])]
    ppermute x4 -> x2, starting transfers between devices: 10.7 us -> 2.7 us  [passed_along(): return lax.ppermute(block, axis, route)]
    ppermute x28 -> x37, starting transfers between devices: 74.3 us -> 66.9 us  [the longest x18 38.3 us: piece_to_space(): return lax.ppermute(block, SPACE, route)]
    pallas_call x6 -> x12, Pallas kernels: 78.7 us -> 85.8 us  [the longest x5 42.1 us: call_density(): pl.pallas_call(functools.partial(density_kernel, pieces, first, turns, ro...]
  transfers between devices with their start and end apart: 32 -> 39, of which waited for: 6 -> 12; matrix products, arithmetic and copies ran while one was open for 4% -> 3% of each run, Pallas kernels for 15% -> 19%
where the time goes in v2:
time: 370 us; the launch traced here: 367 us
  waiting for transfers between devices  177 us (48%)
  Pallas kernels  89.9 us (24%)
  starting transfers between devices  69.6 us (19%)
  local copies, waits for them, and re-layouts  21.5 us (6%)
  other arithmetic  7.37 us (2%)
    ppermute x13, waiting for transfers between devices, swapped(): return lax.ppermute(block, DEV, [(d, d ^ flip) for d in range(n_dev)])  108 us
    ppermute x6, waiting for transfers between devices, piece_turned(): return lax.ppermute(block, (SPACE, DEV), route)  69.2 us
    pallas_call x5, Pallas kernels, call_density(): pl.pallas_call(functools.partial(density_kernel, pieces, first, turns, ro...  42.1 us
    ppermute x18, starting transfers between devices, piece_to_space(): return lax.ppermute(block, SPACE, route)  38.3 us
    pallas_call x4, Pallas kernels, call_potential(): pl.pallas_call(functools.partial(potential_kernel, counts, k, places, chu...  37.5 us
    ppermute x6, starting transfers between devices, piece_turned(): return lax.ppermute(block, (SPACE, DEV), route)  15.3 us
    unnamed x81, local copies, waits for them, and re-layouts  14.7 us
    ppermute x13, starting transfers between devices, swapped(): return lax.ppermute(block, DEV, [(d, d ^ flip) for d in range(n_dev)])  13.2 us
  transfers between devices with their start and end apart: 39, of which 12 were waited for; matrix products, arithmetic and copies ran while one was open for 3% of the time, Pallas kernels for 19%

profile of v2, /device:TPU:0, one launch (start us, length us, event | category | flops | bytes accessed | tf_op | source)
XLA Modules:
  0.0 366.6 jit_solution(8557326632923930702)
XLA Ops:
  2.1 3.1 collective-permute-start.16
  6.8 4.8 %collective-permute-start.7 = (f32[128,1024]{1,0:T(8,128)S(1)}, f32[128,1024]{1,0:T(8,128)S(1)}, u32[]{:S(2)}, u32[]{:S(2)}) collective-permute-start(f32[128,1024]{1,0:T(8,128)S(1)} %get-tuple-element.63), channel_id=1, source_target_pairs={{0,4},{1,5},{2,6},{3,7},{4,0},{5,1},{6,2},{7,3},{8,12},{9,13},{10,... | collective-permute-start | bytes 1572872 | tf_op jit(solution)/shard_map/ppermute | solution.py:451
  13.7 27.2 %collective-permute-done.4 = f32[2,512]{1,0:T(2,128)S(1)} collective-permute-done((f32[2,512]{1,0:T(2,128)S(1)}, f32[2,512]{1,0:T(2,128)S(1)}, u32[]{:S(2)}, u32[]{:S(2)}) %collective-permute-start.4) | collective-permute-done | bytes 4128 | tf_op jit(solution)/shard_map/ppermute | solution.py:425
  43.9 31.3 %collective-permute-done.2 = f32[2,512]{1,0:T(2,128)S(1)} collective-permute-done((f32[2,512]{1,0:T(2,128)S(1)}, f32[2,512]{1,0:T(2,128)S(1)}, u32[]{:S(2)}, u32[]{:S(2)}) %collective-permute-start.2) | collective-permute-done | bytes 4128 | tf_op jit(solution)/shard_map/ppermute | solution.py:425
  77.0 2.7 collective-permute-start.9
  79.9 18.3 %collective-permute-done.17.refs_1_ = f32[1,128,1024]{2,1,0:T(8,128)S(1)} collective-permute-done((f32[1,128,1024]{2,1,0:T(8,128)S(1)}, f32[1,128,1024]{2,1,0:T(8,128)S(1)}, u32[]{:S(2)}, u32[]{:S(2)}) %collective-permute-start.17) | collective-permute-done | bytes 524320 | tf_op jit(solution)/shard_map/ppermute | solution.py:425
  101.1 23.3 %collective-permute-done.9.refs_7_.refs_10_.refs_9_ = f32[128,2048]{1,0:T(8,128)S(1)} collective-permute-done((f32[128,2048]{1,0:T(8,128)S(1)}, f32[128,2048]{1,0:T(8,128)S(1)}, u32[]{:S(2)}, u32[]{:S(2)}) %collective-permute-start.9) | collective-permute-done | bytes 1048608 | tf_op jit(solution)/shard_map/ppermute | solution.py:451
  126.4 20.7 %collective-permute-done.6.refs_1_.refs_2_ = f32[1,384,1024]{2,1,0:T(8,128)} collective-permute-done((f32[1,384,1024]{2,1,0:T(8,128)S(1)}, f32[1,384,1024]{2,1,0:T(8,128)}, u32[]{:S(2)}, u32[]{:S(2)}) %collective-permute-start.6) | collective-permute-done | bytes 1572896 | tf_op jit(solution)/shard_map/ppermute | solution.py:425
  148.8 4.2 %collective-permute-start.10 = (f32[128,2048]{1,0:T(8,128)S(1)}, f32[128,2048]{1,0:T(8,128)}, u32[]{:S(2)}, u32[]{:S(2)}) collective-permute-start(f32[128,2048]{1,0:T(8,128)S(1)} %collective-permute-done.9.refs_7_.refs_10_.refs_9_), channel_id=1, source_target_pairs={{0,8},{8,16},{16,24},{1,9},{9,17},{17,25},{2,10},{10,18},{18,26},{... | collective-permute-start | bytes 3145736 | tf_op jit(solution)/shard_map/ppermute | solution.py:443
  160.0 7.5 %density_rows.5 = (f32[2,1,384]{2,1,0:T(1,128)}, bf16[2,384,1024]{2,1,0:T(8,128)(2,1)}, bf16[2,384,1024]{2,1,0:T(8,128)(2,1)}) custom-call(s32[3]{0:T(128)} %pad_add_fusion.where, s32[16]{0:T(128)} %reshape.19.union, f32[2,384,1024]{2,1,0:T(8,128)} %refs_0_.3, f32[128,4096]{1,0:T(8,128)} %copy-done.13, f32[128,4096]{1,0:T(8,128)} %refs_3_.3, ...), custom_call_target="tpu_custom_call" | custom-call | flops 603979776 | bytes 12582912 | tf_op jit(solution)/shard_map/density_rows/pallas_call | solution.py:295
  169.5 9.1 %density_rows.6 = (f32[3,1,384]{2,1,0:T(1,128)}, bf16[3,384,1024]{2,1,0:T(8,128)(2,1)}, bf16[3,384,1024]{2,1,0:T(8,128)(2,1)}) custom-call(s32[3]{0:T(128)} %pad_add_fusion.where, s32[64]{0:T(128)} %reshape.20.union, f32[2,384,1024]{2,1,0:T(8,128)} %copy-done.16, f32[1,384,1024]{2,1,0:T(8,128)} %collective-permute-done.6.refs_1_.refs_2_, ...), custom_call_target="tpu_custom_call" | custom-call | flops 905969664 | bytes 15728640 | tf_op jit(solution)/shard_map/density_rows/pallas_call | solution.py:295
  178.6 5.3 %collective-permute-done.18.refs_2_ = f32[1,384,1024]{2,1,0:T(8,128)} collective-permute-done((f32[1,384,1024]{2,1,0:T(8,128)}, f32[1,384,1024]{2,1,0:T(8,128)}, u32[]{:S(2)}, u32[]{:S(2)}) %collective-permute-start.18) | collective-permute-done | bytes 1572896 | tf_op jit(solution)/shard_map/ppermute | solution.py:425
  183.9 8.3 %density_rows.8 = (f32[2,1,384]{2,1,0:T(1,128)}, bf16[2,384,1024]{2,1,0:T(8,128)(2,1)}, bf16[2,384,1024]{2,1,0:T(8,128)(2,1)}) custom-call(s32[3]{0:T(128)} %pad_add_fusion.where, s32[64]{0:T(128)} %reshape.20.union, f32[1,256,1024]{2,1,0:T(8,128)} %collective-permute-done.16.refs_0_, f32[1,128,1024]{2,1,0:T(8,128)} %copy-done.25, ...), custom_call_target="tpu_custom_call" | custom-call | flops 1207959552 | bytes 18874368 | tf_op jit(solution)/shard_map/density_rows/pallas_call | solution.py:295
  192.3 12.2 %density_rows.7 = f32[5,1,384]{2,1,0:T(1,128)} custom-call(s32[3]{0:T(128)} %pad_add_fusion.where, s32[64]{0:T(128)} %reshape.20.union, f32[2,384,1024]{2,1,0:T(8,128)} %refs_0_.3, f32[2,384,1024]{2,1,0:T(8,128)} %copy-done.16, f32[1,384,1024]{2,1,0:T(8,128)} %collective-permute-done.6.refs_1_.refs_2_, f32[128,1024]{1,0:T(8,128)} %copy-done.19, ...), custom_call_target="tpu_custom_call" | custom-call | flops 1509949440 | bytes 22020096 | tf_op jit(solution)/shard_map/density_rows/pallas_call | solution.py:295
  208.0 5.0 %density_rows.9 = (f32[1,1,384]{2,1,0:T(1,128)}, bf16[1,384,1024]{2,1,0:T(8,128)(2,1)}, bf16[1,384,1024]{2,1,0:T(8,128)(2,1)}) custom-call(s32[3]{0:T(128)} %pad_add_fusion.where, s32[64]{0:T(128)} %reshape.20.union, f32[1,256,1024]{2,1,0:T(8,128)} %copy-done.23, f32[1,128,1024]{2,1,0:T(8,128)} %copy-done.24, f32[128,4096]{1,0:T(8,128)} %copy-done.13, ...), custom_call_target="tpu_custom_call" | custom-call | flops 603979776 | bytes 15728640 | tf_op jit(solution)/shard_map/density_rows/pallas_call | solution.py:295
  221.0 2.1 potential_net.1.refs_8_
  223.7 9.3 %potential_rows.7 = (f32[128,1024]{1,0:T(8,128)}, f32[128,2048]{1,0:T(8,128)}, f32[128,1024]{1,0:T(8,128)}, f32[128,1024]{1,0:T(8,128)}, f32[128,2048]{1,0:T(8,128)}, /*index=5*/f32[128,1024]{1,0:T(8,128)}) custom-call(s32[3]{0:T(128)} %pad_add_fusion.where, s32[64]{0:T(128)} %reshape.20.union, bf16[2,384,1024]{2,1,0:T(8,128)(2,1)} %get-tuple-element.36.refs_0_, ...), custom_call_target="tpu_custom_call" | custom-call | flops 3221225472 | bytes 16777216 | tf_op jit(solution)/shard_map/potential_rows/pallas_call | solution.py:330
  233.0 4.6 %collective-permute-start.31 = (f32[128,2048]{1,0:T(8,128)}, f32[128,2048]{1,0:T(8,128)S(1)}, u32[]{:S(2)}, u32[]{:S(2)}) collective-permute-start(f32[128,2048]{1,0:T(8,128)} %get-tuple-element.55), channel_id=1, source_target_pairs={{0,8},{8,16},{16,24},{1,9},{9,17},{17,25},{2,10},{10,18},{18,26},{... | collective-permute-start | bytes 3145736 | tf_op jit(solution)/shard_map/ppermute | solution.py:443
  238.9 11.3 %potential_rows.5 = (f32[128,1024]{1,0:T(8,128)}, f32[128,2048]{1,0:T(8,128)}, f32[128,1024]{1,0:T(8,128)}, f32[128,1024]{1,0:T(8,128)}, f32[128,2048]{1,0:T(8,128)}, /*index=5*/f32[128,1024]{1,0:T(8,128)}) custom-call(s32[3]{0:T(128)} %pad_add_fusion.where, s32[64]{0:T(128)} %reshape.20.union, bf16[2,384,1024]{2,1,0:T(8,128)(2,1)} %get-tuple-element.36.refs_0_, ...), custom_call_target="tpu_custom_call" | custom-call | flops 3221225472 | bytes 16777216 | tf_op jit(solution)/shard_map/potential_rows/pallas_call | solution.py:330
  252.2 5.9 %collective-permute-start.34 = (f32[128,1024]{1,0:T(8,128)}, f32[128,1024]{1,0:T(8,128)}, u32[]{:S(2)}, u32[]{:S(2)}) collective-permute-start(f32[128,1024]{1,0:T(8,128)} %get-tuple-element.58), channel_id=1, source_target_pairs={{0,8},{8,16},{1,9},{9,17},{2,10},{10,18},{3,11},{11,19},{4,12},{12... | collective-permute-start | bytes 1572872 | tf_op jit(solution)/shard_map/ppermute | solution.py:443
  258.1 7.8 %potential_rows.6 = (f32[128,1024]{1,0:T(8,128)}, f32[128,2048]{1,0:T(8,128)}, f32[128,1024]{1,0:T(8,128)}) custom-call(s32[3]{0:T(128)} %pad_add_fusion.where, s32[64]{0:T(128)} %reshape.20.union, bf16[2,384,1024]{2,1,0:T(8,128)(2,1)} %get-tuple-element.36.refs_0_, bf16[2,384,1024]{2,1,0:T(8,128)(2,1)} %get-tuple-element.37.refs_1_, ...), custom_call_target="tpu_custom_call" | custom-call | flops 1610612736 | bytes 14680064 | tf_op jit(solution)/shard_map/potential_rows/pallas_call | solution.py:330
  268.7 2.5 add_add_fusion
  273.3 6.2 %collective-permute-start.27 = (f32[128,1024]{1,0:T(8,128)S(1)}, f32[128,1024]{1,0:T(8,128)S(1)}, u32[]{:S(2)}, u32[]{:S(2)}) collective-permute-start(f32[128,1024]{1,0:T(8,128)S(1)} %copy-done.39), channel_id=1, source_target_pairs={{0,8},{8,16},{1,9},{9,17},{2,10},{10,18},{3,11},{11,19},{4,12},{12... | collective-permute-start | bytes 1572872 | tf_op jit(solution)/shard_map/ppermute | solution.py:443
  279.5 4.3 %collective-permute-start.28 = (f32[128,2048]{1,0:T(8,128)}, f32[128,2048]{1,0:T(8,128)S(1)}, u32[]{:S(2)}, u32[]{:S(2)}) collective-permute-start(f32[128,2048]{1,0:T(8,128)} %get-tuple-element.51), channel_id=1, source_target_pairs={{0,8},{8,16},{16,24},{1,9},{9,17},{17,25},{2,10},{10,18},{18,26},{... | collective-permute-start | bytes 3145736 | tf_op jit(solution)/shard_map/ppermute | solution.py:443
  284.7 2.0 add_add_fusion.2
  288.3 4.8 %collective-permute-start.35 = (f32[128,1024]{1,0:T(8,128)}, f32[128,1024]{1,0:T(8,128)}, u32[]{:S(2)}, u32[]{:S(2)}) collective-permute-start(f32[128,1024]{1,0:T(8,128)} %add_add_fusion.2), channel_id=1, source_target_pairs={{0,4},{1,5},{2,6},{3,7},{4,0},{5,1},{6,2},{7,3},{8,12},{9,13},{10,... | collective-permute-start | bytes 1572872 | tf_op jit(solution)/shard_map/ppermute | solution.py:451
  295.4 9.1 %potential_rows.4 = (f32[128,1024]{1,0:T(8,128)}, f32[128,2048]{1,0:T(8,128)}, f32[128,1024]{1,0:T(8,128)}) custom-call(s32[3]{0:T(128)} %pad_add_fusion.where, s32[64]{0:T(128)} %reshape.20.union, bf16[2,384,1024]{2,1,0:T(8,128)(2,1)} %get-tuple-element.36.refs_0_, bf16[2,384,1024]{2,1,0:T(8,128)(2,1)} %get-tuple-element.37.refs_1_, ...), custom_call_target="tpu_custom_call" | custom-call | flops 1610612736 | bytes 14680064 | tf_op jit(solution)/shard_map/potential_rows/pallas_call | solution.py:330
  314.5 36.6 %collective-permute-done.32.term_ref = f32[128,2048]{1,0:T(8,128)S(1)} collective-permute-done((f32[128,2048]{1,0:T(8,128)}, f32[128,2048]{1,0:T(8,128)S(1)}, u32[]{:S(2)}, u32[]{:S(2)}) %collective-permute-start.32) | collective-permute-done | bytes 1048608 | tf_op jit(solution)/shard_map/ppermute | solution.py:451
  351.1 2.1 added_rows.3.sum_ref
  353.2 9.3 %collective-permute-done.35.term_ref = f32[128,1024]{1,0:T(8,128)} collective-permute-done((f32[128,1024]{1,0:T(8,128)}, f32[128,1024]{1,0:T(8,128)}, u32[]{:S(2)}, u32[]{:S(2)}) %collective-permute-start.35) | collective-permute-done | bytes 524320 | tf_op jit(solution)/shard_map/ppermute | solution.py:451
  362.5 2.0 added_rows.4.sum_ref
  364.5 2.0 added_rows.5
  (166 shorter events, 60.1 us)
Async XLA Ops:
  2.1 97.5 %collective-permute-start.16 = (f32[1,256,1024]{2,1,0:T(8,128)S(1)}, f32[1,256,1024]{2,1,0:T(8,128)}, u32[]{:S(2)}, u32[]{:S(2)}) collective-permute-start(f32[1,256,1024]{2,1,0:T(8,128)S(1)} %slice.35), channel_id=1, source_target_pairs={{0,2},{1,3},{2,0},{3,1},{4,6},{5,7},{6,4},{7,5},{8,10},{9,11},{10,... | collective-permute-start | bytes 3145736 | tf_op jit(solution)/shard_map/ppermute | solution.py:425
  5.2 150.4 %collective-permute-start.5 = (f32[2,384,1024]{2,1,0:T(8,128)}, f32[2,384,1024]{2,1,0:T(8,128)S(1)}, u32[]{:S(2)}, u32[]{:S(2)}) collective-permute-start(f32[2,384,1024]{2,1,0:T(8,128)} %refs_0_.3), channel_id=1, source_target_pairs={{0,1},{1,0},{2,3},{3,2},{4,5},{5,4},{6,7},{7,6},{8,9},{9,8},{10,11... | collective-permute-start | bytes 9437192 | tf_op jit(solution)/shard_map/ppermute | solution.py:425
  6.8 68.7 %collective-permute-start.7 = (f32[128,1024]{1,0:T(8,128)S(1)}, f32[128,1024]{1,0:T(8,128)S(1)}, u32[]{:S(2)}, u32[]{:S(2)}) collective-permute-start(f32[128,1024]{1,0:T(8,128)S(1)} %get-tuple-element.63), channel_id=1, source_target_pairs={{0,4},{1,5},{2,6},{3,7},{4,0},{5,1},{6,2},{7,3},{8,12},{9,13},{10,... | collective-permute-start | bytes 1572872 | tf_op jit(solution)/shard_map/ppermute | solution.py:451
  11.7 29.3 %collective-permute-start.4 = (f32[2,512]{1,0:T(2,128)S(1)}, f32[2,512]{1,0:T(2,128)S(1)}, u32[]{:S(2)}, u32[]{:S(2)}) collective-permute-start(f32[2,512]{1,0:T(2,128)S(1)} %select_maximum_fusion), channel_id=1, source_target_pairs={{0,3},{1,2},{2,1},{3,0},{4,7},{5,6},{6,5},{7,4},{8,11},{9,10},{10,... | collective-permute-start | bytes 12296 | tf_op jit(solution)/shard_map/ppermute | solution.py:425
  12.1 29.2 %collective-permute-start.3 = (f32[2,512]{1,0:T(2,128)S(1)}, f32[2,512]{1,0:T(2,128)S(1)}, u32[]{:S(2)}, u32[]{:S(2)}) collective-permute-start(f32[2,512]{1,0:T(2,128)S(1)} %select_maximum_fusion), channel_id=1, source_target_pairs={{0,2},{1,3},{2,0},{3,1},{4,6},{5,7},{6,4},{7,5},{8,10},{9,11},{10,... | collective-permute-start | bytes 12296 | tf_op jit(solution)/shard_map/ppermute | solution.py:425
  40.9 34.2 %collective-permute-start.2 = (f32[2,512]{1,0:T(2,128)S(1)}, f32[2,512]{1,0:T(2,128)S(1)}, u32[]{:S(2)}, u32[]{:S(2)}) collective-permute-start(f32[2,512]{1,0:T(2,128)S(1)} %select_maximum_fusion), channel_id=1, source_target_pairs={{0,1},{1,0},{2,3},{3,2},{4,5},{5,4},{6,7},{7,6},{8,9},{9,8},{10,11... | collective-permute-start | bytes 12296 | tf_op jit(solution)/shard_map/ppermute | solution.py:425
  41.3 35.7 %collective-permute-start.11 = (f32[128,1024]{1,0:T(8,128)S(1)}, f32[128,1024]{1,0:T(8,128)}, u32[]{:S(2)}, u32[]{:S(2)}) collective-permute-start(f32[128,1024]{1,0:T(8,128)S(1)} %get-tuple-element.62), channel_id=1, source_target_pairs={{8,12},{9,13},{10,14},{11,15},{12,8},{13,9},{14,10},{15,11},{16,20... | collective-permute-start | bytes 1572872 | tf_op jit(solution)/shard_map/ppermute | solution.py:451
  75.2 23.1 %collective-permute-start.17 = (f32[1,128,1024]{2,1,0:T(8,128)S(1)}, f32[1,128,1024]{2,1,0:T(8,128)S(1)}, u32[]{:S(2)}, u32[]{:S(2)}) collective-permute-start(f32[1,128,1024]{2,1,0:T(8,128)S(1)} %slice.36), channel_id=1, source_target_pairs={{0,2},{1,3},{2,0},{3,1},{4,6},{5,7},{6,4},{7,5},{8,10},{9,11},{10,... | collective-permute-start | bytes 1572872 | tf_op jit(solution)/shard_map/ppermute | solution.py:425
  75.5 24.2 %collective-permute-start.8 = (f32[128,1024]{1,0:T(8,128)S(1)}, f32[128,1024]{1,0:T(8,128)S(1)}, u32[]{:S(2)}, u32[]{:S(2)}) collective-permute-start(f32[128,1024]{1,0:T(8,128)S(1)} %collective-permute-done.7.refs_6_.refs_9_.refs_8_), channel_id=1, source_target_pairs={{0,8},{1,9},{2,10},{3,11},{4,12},{5,13},{6,14},{7,15}} | collective-permute-start | bytes 1572872 | tf_op jit(solution)/shard_map/ppermute | solution.py:443
  77.0 47.3 %collective-permute-start.9 = (f32[128,2048]{1,0:T(8,128)S(1)}, f32[128,2048]{1,0:T(8,128)S(1)}, u32[]{:S(2)}, u32[]{:S(2)}) collective-permute-start(f32[128,2048]{1,0:T(8,128)S(1)} %slice.33), channel_id=1, source_target_pairs={{0,4},{1,5},{2,6},{3,7},{4,0},{5,1},{6,2},{7,3},{8,12},{9,13},{10,... | collective-permute-start | bytes 3145736 | tf_op jit(solution)/shard_map/ppermute | solution.py:451
  98.2 54.7 %collective-permute-start = (f32[128,4096]{1,0:T(8,128)S(1)}, f32[128,4096]{1,0:T(8,128)S(1)}, u32[]{:S(2)}, u32[]{:S(2)}) collective-permute-start(f32[128,4096]{1,0:T(8,128)S(1)} %copy-done.12), channel_id=1, source_target_pairs={{0,8},{8,16},{16,24},{1,9},{9,17},{17,25},{2,10},{10,18},{18,26},{... | collective-permute-start | bytes 6291464 | tf_op jit(solution)/shard_map/ppermute | solution.py:23
  99.7 47.4 %collective-permute-start.6 = (f32[1,384,1024]{2,1,0:T(8,128)S(1)}, f32[1,384,1024]{2,1,0:T(8,128)}, u32[]{:S(2)}, u32[]{:S(2)}) collective-permute-start(f32[1,384,1024]{2,1,0:T(8,128)S(1)} %slice.31), channel_id=1, source_target_pairs={{0,2},{1,3},{2,0},{3,1},{4,6},{5,7},{6,4},{7,5},{8,10},{9,11},{10,... | collective-permute-start | bytes 4718600 | tf_op jit(solution)/shard_map/ppermute | solution.py:425
  99.8 54.5 %collective-permute-start.1 = (f32[128,4096]{1,0:T(8,128)S(1)}, f32[128,4096]{1,0:T(8,128)S(1)}, u32[]{:S(2)}, u32[]{:S(2)}) collective-permute-start(f32[128,4096]{1,0:T(8,128)S(1)} %copy-done.12), channel_id=1, source_target_pairs={{8,0},{16,8},{24,16},{9,1},{17,9},{25,17},{10,2},{18,10},{26,18},{... | collective-permute-start | bytes 6291464 | tf_op jit(solution)/shard_map/ppermute | solution.py:23
  125.1 23.7 %collective-permute-start.13 = (f32[128,1024]{1,0:T(8,128)S(1)}, f32[128,1024]{1,0:T(8,128)S(1)}, u32[]{:S(2)}, u32[]{:S(2)}) collective-permute-start(f32[128,1024]{1,0:T(8,128)S(1)} %collective-permute-done.7.refs_6_.refs_9_.refs_8_), channel_id=1, source_target_pairs={{8,0},{16,8},{9,1},{17,9},{10,2},{18,10},{11,3},{19,11},{12,4},{20... | collective-permute-start | bytes 1572872 | tf_op jit(solution)/shard_map/ppermute | solution.py:443
  147.1 36.8 %collective-permute-start.18 = (f32[1,384,1024]{2,1,0:T(8,128)}, f32[1,384,1024]{2,1,0:T(8,128)}, u32[]{:S(2)}, u32[]{:S(2)}) collective-permute-start(f32[1,384,1024]{2,1,0:T(8,128)} %collective-permute-done.6.refs_1_.refs_2_), channel_id=1, source_target_pairs={{0,1},{1,0},{2,3},{3,2},{4,5},{5,4},{6,7},{7,6},{8,9},{9,8},{10,11... | collective-permute-start | bytes 4718600 | tf_op jit(solution)/shard_map/ppermute | solution.py:425
  148.8 29.8 %collective-permute-start.10 = (f32[128,2048]{1,0:T(8,128)S(1)}, f32[128,2048]{1,0:T(8,128)}, u32[]{:S(2)}, u32[]{:S(2)}) collective-permute-start(f32[128,2048]{1,0:T(8,128)S(1)} %collective-permute-done.9.refs_7_.refs_10_.refs_9_), channel_id=1, source_target_pairs={{0,8},{8,16},{16,24},{1,9},{9,17},{17,25},{2,10},{10,18},{18,26},{... | collective-permute-start | bytes 3145736 | tf_op jit(solution)/shard_map/ppermute | solution.py:443
  153.0 25.6 %collective-permute-start.14 = (f32[128,2048]{1,0:T(8,128)S(1)}, f32[128,2048]{1,0:T(8,128)}, u32[]{:S(2)}, u32[]{:S(2)}) collective-permute-start(f32[128,2048]{1,0:T(8,128)S(1)} %collective-permute-done.9.refs_7_.refs_10_.refs_9_), channel_id=1, source_target_pairs={{8,0},{16,8},{24,16},{9,1},{17,9},{25,17},{10,2},{18,10},{26,18},{... | collective-permute-start | bytes 3145736 | tf_op jit(solution)/shard_map/ppermute | solution.py:443
  154.3 15.2 %collective-permute-start.15 = (f32[128,1024]{1,0:T(8,128)}, f32[128,1024]{1,0:T(8,128)S(1)}, u32[]{:S(2)}, u32[]{:S(2)}) collective-permute-start(f32[128,1024]{1,0:T(8,128)} %collective-permute-done.11.refs_8_.refs_11_.refs_10_), channel_id=1, source_target_pairs={{24,16},{25,17},{26,18},{27,19},{28,20},{29,21},{30,22},{31,23}} | collective-permute-start | bytes 1572872 | tf_op jit(solution)/shard_map/ppermute | solution.py:443
  157.3 49.0 %collective-permute-start.19 = (f32[1,256,1024]{2,1,0:T(8,128)}, f32[1,256,1024]{2,1,0:T(8,128)S(1)}, u32[]{:S(2)}, u32[]{:S(2)}) collective-permute-start(f32[1,256,1024]{2,1,0:T(8,128)} %collective-permute-done.16.refs_0_), channel_id=1, source_target_pairs={{0,1},{1,0},{2,3},{3,2},{4,5},{5,4},{6,7},{7,6},{8,9},{9,8},{10,11... | collective-permute-start | bytes 3145736 | tf_op jit(solution)/shard_map/ppermute | solution.py:425
  169.5 36.8 %collective-permute-start.20 = (f32[1,128,1024]{2,1,0:T(8,128)}, f32[1,128,1024]{2,1,0:T(8,128)S(1)}, u32[]{:S(2)}, u32[]{:S(2)}) collective-permute-start(f32[1,128,1024]{2,1,0:T(8,128)} %slice.40), channel_id=1, source_target_pairs={{0,2},{1,3},{2,0},{3,1},{4,6},{5,7},{6,4},{7,5},{8,10},{9,11},{10,... | collective-permute-start | bytes 1572872 | tf_op jit(solution)/shard_map/ppermute | solution.py:425
  233.0 34.2 %collective-permute-start.31 = (f32[128,2048]{1,0:T(8,128)}, f32[128,2048]{1,0:T(8,128)S(1)}, u32[]{:S(2)}, u32[]{:S(2)}) collective-permute-start(f32[128,2048]{1,0:T(8,128)} %get-tuple-element.55), channel_id=1, source_target_pairs={{0,8},{8,16},{16,24},{1,9},{9,17},{17,25},{2,10},{10,18},{18,26},{... | collective-permute-start | bytes 3145736 | tf_op jit(solution)/shard_map/ppermute | solution.py:443
  237.6 30.4 %collective-permute-start.30 = (f32[128,2048]{1,0:T(8,128)}, f32[128,2048]{1,0:T(8,128)S(1)}, u32[]{:S(2)}, u32[]{:S(2)}) collective-permute-start(f32[128,2048]{1,0:T(8,128)} %get-tuple-element.54), channel_id=1, source_target_pairs={{8,0},{16,8},{24,16},{9,1},{17,9},{25,17},{10,2},{18,10},{26,18},{... | collective-permute-start | bytes 3145736 | tf_op jit(solution)/shard_map/ppermute | solution.py:443
  250.2 15.7 %collective-permute-start.24 = (f32[128,1024]{1,0:T(8,128)}, f32[128,1024]{1,0:T(8,128)S(1)}, u32[]{:S(2)}, u32[]{:S(2)}) collective-permute-start(f32[128,1024]{1,0:T(8,128)} %get-tuple-element.47), channel_id=1, source_target_pairs={{8,0},{9,1},{10,2},{11,3},{12,4},{13,5},{14,6},{15,7}} | collective-permute-start | bytes 1572872 | tf_op jit(solution)/shard_map/ppermute | solution.py:443
  251.5 19.7 %collective-permute-start.26 = (f32[128,1024]{1,0:T(8,128)}, f32[128,1024]{1,0:T(8,128)S(1)}, u32[]{:S(2)}, u32[]{:S(2)}) collective-permute-start(f32[128,1024]{1,0:T(8,128)} %get-tuple-element.49), channel_id=1, source_target_pairs={{16,8},{24,16},{17,9},{25,17},{18,10},{26,18},{19,11},{27,19},{20,... | collective-permute-start | bytes 1572872 | tf_op jit(solution)/shard_map/ppermute | solution.py:443
  252.2 21.1 %collective-permute-start.34 = (f32[128,1024]{1,0:T(8,128)}, f32[128,1024]{1,0:T(8,128)}, u32[]{:S(2)}, u32[]{:S(2)}) collective-permute-start(f32[128,1024]{1,0:T(8,128)} %get-tuple-element.58), channel_id=1, source_target_pairs={{0,8},{8,16},{1,9},{9,17},{2,10},{10,18},{3,11},{11,19},{4,12},{12... | collective-permute-start | bytes 1572872 | tf_op jit(solution)/shard_map/ppermute | solution.py:443
  267.3 16.6 %collective-permute-start.37 = (f32[128,1024]{1,0:T(8,128)}, f32[128,1024]{1,0:T(8,128)S(1)}, u32[]{:S(2)}, u32[]{:S(2)}) collective-permute-start(f32[128,1024]{1,0:T(8,128)} %get-tuple-element.61), channel_id=1, source_target_pairs={{16,24},{17,25},{18,26},{19,27},{20,28},{21,29},{22,30},{23,31}} | collective-permute-start | bytes 1572872 | tf_op jit(solution)/shard_map/ppermute | solution.py:443
  268.0 16.6 %collective-permute-start.36 = (f32[128,1024]{1,0:T(8,128)}, f32[128,1024]{1,0:T(8,128)S(1)}, u32[]{:S(2)}, u32[]{:S(2)}) collective-permute-start(f32[128,1024]{1,0:T(8,128)} %get-tuple-element.60), channel_id=1, source_target_pairs={{16,8},{24,16},{17,9},{25,17},{18,10},{26,18},{19,11},{27,19},{20,... | collective-permute-start | bytes 1572872 | tf_op jit(solution)/shard_map/ppermute | solution.py:443
  272.0 33.1 %collective-permute-start.25 = (f32[128,2048]{1,0:T(8,128)}, f32[128,2048]{1,0:T(8,128)S(1)}, u32[]{:S(2)}, u32[]{:S(2)}) collective-permute-start(f32[128,2048]{1,0:T(8,128)} %get-tuple-element.48), channel_id=1, source_target_pairs={{8,0},{16,8},{24,16},{9,1},{17,9},{25,17},{10,2},{18,10},{26,18},{... | collective-permute-start | bytes 3145736 | tf_op jit(solution)/shard_map/ppermute | solution.py:443
  279.5 25.6 %collective-permute-start.28 = (f32[128,2048]{1,0:T(8,128)}, f32[128,2048]{1,0:T(8,128)S(1)}, u32[]{:S(2)}, u32[]{:S(2)}) collective-permute-start(f32[128,2048]{1,0:T(8,128)} %get-tuple-element.51), channel_id=1, source_target_pairs={{0,8},{8,16},{16,24},{1,9},{9,17},{17,25},{2,10},{10,18},{18,26},{... | collective-permute-start | bytes 3145736 | tf_op jit(solution)/shard_map/ppermute | solution.py:443
  284.6 66.5 %collective-permute-start.32 = (f32[128,2048]{1,0:T(8,128)}, f32[128,2048]{1,0:T(8,128)S(1)}, u32[]{:S(2)}, u32[]{:S(2)}) collective-permute-start(f32[128,2048]{1,0:T(8,128)} %add_add_fusion), channel_id=1, source_target_pairs={{0,4},{1,5},{2,6},{3,7},{4,0},{5,1},{6,2},{7,3},{8,12},{9,13},{10,... | collective-permute-start | bytes 3145736 | tf_op jit(solution)/shard_map/ppermute | solution.py:451
  288.3 74.1 %collective-permute-start.35 = (f32[128,1024]{1,0:T(8,128)}, f32[128,1024]{1,0:T(8,128)}, u32[]{:S(2)}, u32[]{:S(2)}) collective-permute-start(f32[128,1024]{1,0:T(8,128)} %add_add_fusion.2), channel_id=1, source_target_pairs={{0,4},{1,5},{2,6},{3,7},{4,0},{5,1},{6,2},{7,3},{8,12},{9,13},{10,... | collective-permute-start | bytes 1572872 | tf_op jit(solution)/shard_map/ppermute | solution.py:451
  294.0 70.6 %collective-permute-start.38 = (f32[128,1024]{1,0:T(8,128)}, f32[128,1024]{1,0:T(8,128)}, u32[]{:S(2)}, u32[]{:S(2)}) collective-permute-start(f32[128,1024]{1,0:T(8,128)} %add_add_fusion.1), channel_id=1, source_target_pairs={{8,12},{9,13},{10,14},{11,15},{12,8},{13,9},{14,10},{15,11},{16,20... | collective-permute-start | bytes 1572872 | tf_op jit(solution)/shard_map/ppermute | solution.py:451
  (47 other events, 936.3 us)

commit v3 on v2

--- a/solution.py
+++ b/solution.py
@@ -207,12 +207,11 @@
     n_halves = 2 * len(counts)
     half_refs, scale_ref, out_refs = refs[:n_halves], refs[n_halves], refs[n_halves + 1 : -5]
     sums, term, highs, lows, sems = refs[-5:]
-    copies = []
     for n, half_ref in enumerate(half_refs):
-        at = pl.ds(sum(counts[: n // 2]), counts[n // 2])
-        held = (highs, lows)[n % 2].at[at]
-        copies.append(pltpu.make_async_copy(half_ref, held, sems.at[n]))
-        copies[-1].start()
+        for b in range(counts[n // 2]):
+            batch = sum(counts[: n // 2]) + b
+            held = (highs, lows)[n % 2].at[batch]
+            pltpu.make_async_copy(half_ref.at[b], held, sems.at[n % 2, batch]).start()
     sums[...] = jnp.zeros_like(sums)
 
     def add_row(batch, i, slot):
@@ -226,13 +225,14 @@
             at = tile_at(union[batch * U + j])
             sums[slot, :, at] += term[:, j * TILE : (j + 1) * TILE]
 
-    for n, count in enumerate(counts):
-        for copy in copies[2 * n : 2 * n + 2]:
-            copy.wait()
-
-        @pl.loop(sum(counts[:n]) * U, sum(counts[: n + 1]) * U)
-        def _(at):
-            batch, i = at // U, at % U
+    @pl.loop(0, sum(counts))
+    def _(batch):
+        for n, held in enumerate((highs, lows)):
+            block = held.at[batch]
+            pltpu.make_async_copy(block, block, sems.at[n, batch]).wait()
+
+        @pl.loop(0, U)
+        def _(i):
             mine, turn, place = place_of(union[batch * U + i], where, region_tiles)
             wanted = functools.reduce(jnp.logical_or, [place == r for r in places])
 
@@ -339,7 +339,7 @@
             pltpu.VMEM((TILE, width), jnp.float32),
             pltpu.VMEM((sum(counts), points, width), jnp.bfloat16),
             pltpu.VMEM((sum(counts), points, width), jnp.bfloat16),
-            pltpu.SemaphoreType.DMA((len(halves),)),
+            pltpu.SemaphoreType.DMA((2, sum(counts))),
         ],
         cost_estimate=pl.CostEstimate(
             flops=2 * len(places) * sum(counts) * points * width * width // QUAD,
@@ -347,6 +347,7 @@
             + 4 * len(places) * TILE * chunks[-1][1],
             transcendentals=0,
         ),
+        compiler_params=pltpu.CompilerParams(vmem_limit_bytes=44 * 2**20),
         name="potential_rows",
     )(where, union, *halves, scale)
 

time: 370 us -> 365 us (0.986)
  Pallas kernels: 89.9 us -> 77.7 us
  waiting for transfers between devices: 177 us -> 188 us
  local copies, waits for them, and re-layouts: 21.5 us -> 16.3 us
    ppermute x6, waiting for transfers between devices: 69.2 us -> 82.4 us  [piece_turned(): return lax.ppermute(block, (SPACE, DEV), route)]
    pallas_call x4, Pallas kernels: 37.5 us -> 25.6 us  [call_potential(): pl.pallas_call(functools.partial(potential_kernel, counts, k, places, chu...]
    unnamed x81 -> x67, local copies, waits for them, and re-layouts: 14.7 us -> 6.91 us
  transfers between devices with their start and end apart: 39 -> 39, of which waited for: 12 -> 12; matrix products, arithmetic and copies ran while one was open for 3% -> 4% of each run, Pallas kernels for 19% -> 17%
where the time goes in v3:
time: 365 us; the launch traced here: 362 us
  waiting for transfers between devices  188 us (52%)
  Pallas kernels  77.7 us (21%)
  starting transfers between devices  69.6 us (19%)
  local copies, waits for them, and re-layouts  16.3 us (4%)
  other arithmetic  8.44 us (2%)
    ppermute x13, waiting for transfers between devices, swapped(): return lax.ppermute(block, DEV, [(d, d ^ flip) for d in range(n_dev)])  106 us
    ppermute x6, waiting for transfers between devices, piece_turned(): return lax.ppermute(block, (SPACE, DEV), route)  82.4 us
    pallas_call x5, Pallas kernels, call_density(): pl.pallas_call(functools.partial(density_kernel, pieces, first, turns, ro...  42.1 us
    ppermute x18, starting transfers between devices, piece_to_space(): return lax.ppermute(block, SPACE, route)  39.2 us
    pallas_call x4, Pallas kernels, call_potential(): pl.pallas_call(functools.partial(potential_kernel, counts, k, places, chu...  25.6 us
    ppermute x6, starting transfers between devices, piece_turned(): return lax.ppermute(block, (SPACE, DEV), route)  14.6 us
    ppermute x13, starting transfers between devices, swapped(): return lax.ppermute(block, DEV, [(d, d ^ flip) for d in range(n_dev)])  13.2 us
  transfers between devices with their start and end apart: 39, of which 12 were waited for; matrix products, arithmetic and copies ran while one was open for 4% of the time, Pallas kernels for 17%

profile of v3, /device:TPU:0, one launch (start us, length us, event | category | flops | bytes accessed | tf_op | source)
XLA Modules:
  0.0 361.5 jit_solution(764714087034454573)
XLA Ops:
  2.1 3.1 collective-permute-start.16
  6.8 4.8 %collective-permute-start.7 = (f32[128,1024]{1,0:T(8,128)S(1)}, f32[128,1024]{1,0:T(8,128)S(1)}, u32[]{:S(2)}, u32[]{:S(2)}) collective-permute-start(f32[128,1024]{1,0:T(8,128)S(1)} %get-tuple-element.63), channel_id=1, source_target_pairs={{0,4},{1,5},{2,6},{3,7},{4,0},{5,1},{6,2},{7,3},{8,12},{9,13},{10,... | collective-permute-start | bytes 1572872 | tf_op jit(solution)/shard_map/ppermute | solution.py:452
  13.7 27.2 %collective-permute-done.4 = f32[2,512]{1,0:T(2,128)S(1)} collective-permute-done((f32[2,512]{1,0:T(2,128)S(1)}, f32[2,512]{1,0:T(2,128)S(1)}, u32[]{:S(2)}, u32[]{:S(2)}) %collective-permute-start.4) | collective-permute-done | bytes 4128 | tf_op jit(solution)/shard_map/ppermute | solution.py:426
  43.9 31.3 %collective-permute-done.2 = f32[2,512]{1,0:T(2,128)S(1)} collective-permute-done((f32[2,512]{1,0:T(2,128)S(1)}, f32[2,512]{1,0:T(2,128)S(1)}, u32[]{:S(2)}, u32[]{:S(2)}) %collective-permute-start.2) | collective-permute-done | bytes 4128 | tf_op jit(solution)/shard_map/ppermute | solution.py:426
  77.0 2.7 collective-permute-start.9
  79.9 18.3 %collective-permute-done.17.refs_1_ = f32[1,128,1024]{2,1,0:T(8,128)S(1)} collective-permute-done((f32[1,128,1024]{2,1,0:T(8,128)S(1)}, f32[1,128,1024]{2,1,0:T(8,128)S(1)}, u32[]{:S(2)}, u32[]{:S(2)}) %collective-permute-start.17) | collective-permute-done | bytes 524320 | tf_op jit(solution)/shard_map/ppermute | solution.py:426
  101.1 23.3 %collective-permute-done.9.refs_7_.refs_10_.refs_9_ = f32[128,2048]{1,0:T(8,128)S(1)} collective-permute-done((f32[128,2048]{1,0:T(8,128)S(1)}, f32[128,2048]{1,0:T(8,128)S(1)}, u32[]{:S(2)}, u32[]{:S(2)}) %collective-permute-start.9) | collective-permute-done | bytes 1048608 | tf_op jit(solution)/shard_map/ppermute | solution.py:452
  126.4 20.8 %collective-permute-done.6.refs_1_.refs_2_ = f32[1,384,1024]{2,1,0:T(8,128)} collective-permute-done((f32[1,384,1024]{2,1,0:T(8,128)S(1)}, f32[1,384,1024]{2,1,0:T(8,128)}, u32[]{:S(2)}, u32[]{:S(2)}) %collective-permute-start.6) | collective-permute-done | bytes 1572896 | tf_op jit(solution)/shard_map/ppermute | solution.py:426
  148.8 4.2 %collective-permute-start.10 = (f32[128,2048]{1,0:T(8,128)S(1)}, f32[128,2048]{1,0:T(8,128)}, u32[]{:S(2)}, u32[]{:S(2)}) collective-permute-start(f32[128,2048]{1,0:T(8,128)S(1)} %collective-permute-done.9.refs_7_.refs_10_.refs_9_), channel_id=1, source_target_pairs={{0,8},{8,16},{16,24},{1,9},{9,17},{17,25},{2,10},{10,18},{18,26},{... | collective-permute-start | bytes 3145736 | tf_op jit(solution)/shard_map/ppermute | solution.py:444
  161.1 7.3 %density_rows.5 = (f32[2,1,384]{2,1,0:T(1,128)}, bf16[2,384,1024]{2,1,0:T(8,128)(2,1)}, bf16[2,384,1024]{2,1,0:T(8,128)(2,1)}) custom-call(s32[3]{0:T(128)} %pad_add_fusion.where, s32[16]{0:T(128)} %reshape.19.union, f32[2,384,1024]{2,1,0:T(8,128)} %refs_0_.3, f32[128,4096]{1,0:T(8,128)} %copy-done.10, f32[128,4096]{1,0:T(8,128)} %refs_3_.3, ...), custom_call_target="tpu_custom_call" | custom-call | flops 603979776 | bytes 12582912 | tf_op jit(solution)/shard_map/density_rows/pallas_call | solution.py:295
  170.3 9.1 %density_rows.6 = (f32[3,1,384]{2,1,0:T(1,128)}, bf16[3,384,1024]{2,1,0:T(8,128)(2,1)}, bf16[3,384,1024]{2,1,0:T(8,128)(2,1)}) custom-call(s32[3]{0:T(128)} %pad_add_fusion.where, s32[64]{0:T(128)} %reshape.20.union, f32[2,384,1024]{2,1,0:T(8,128)} %copy-done.13, f32[1,384,1024]{2,1,0:T(8,128)} %collective-permute-done.6.refs_1_.refs_2_, ...), custom_call_target="tpu_custom_call" | custom-call | flops 905969664 | bytes 15728640 | tf_op jit(solution)/shard_map/density_rows/pallas_call | solution.py:295
  179.5 4.4 %collective-permute-done.18.refs_2_ = f32[1,384,1024]{2,1,0:T(8,128)} collective-permute-done((f32[1,384,1024]{2,1,0:T(8,128)}, f32[1,384,1024]{2,1,0:T(8,128)}, u32[]{:S(2)}, u32[]{:S(2)}) %collective-permute-start.18) | collective-permute-done | bytes 1572896 | tf_op jit(solution)/shard_map/ppermute | solution.py:426
  183.9 8.3 %density_rows.8 = (f32[2,1,384]{2,1,0:T(1,128)}, bf16[2,384,1024]{2,1,0:T(8,128)(2,1)}, bf16[2,384,1024]{2,1,0:T(8,128)(2,1)}) custom-call(s32[3]{0:T(128)} %pad_add_fusion.where, s32[64]{0:T(128)} %reshape.20.union, f32[1,256,1024]{2,1,0:T(8,128)} %collective-permute-done.16.refs_0_, f32[1,128,1024]{2,1,0:T(8,128)} %copy-done.20, ...), custom_call_target="tpu_custom_call" | custom-call | flops 1207959552 | bytes 18874368 | tf_op jit(solution)/shard_map/density_rows/pallas_call | solution.py:295
  192.3 12.2 %density_rows.7 = f32[5,1,384]{2,1,0:T(1,128)} custom-call(s32[3]{0:T(128)} %pad_add_fusion.where, s32[64]{0:T(128)} %reshape.20.union, f32[2,384,1024]{2,1,0:T(8,128)} %refs_0_.3, f32[2,384,1024]{2,1,0:T(8,128)} %copy-done.13, f32[1,384,1024]{2,1,0:T(8,128)} %collective-permute-done.6.refs_1_.refs_2_, f32[128,1024]{1,0:T(8,128)} %copy-done.16, ...), custom_call_target="tpu_custom_call" | custom-call | flops 1509949440 | bytes 22020096 | tf_op jit(solution)/shard_map/density_rows/pallas_call | solution.py:295
  206.4 5.1 %density_rows.9 = (f32[1,1,384]{2,1,0:T(1,128)}, bf16[1,384,1024]{2,1,0:T(8,128)(2,1)}, bf16[1,384,1024]{2,1,0:T(8,128)(2,1)}) custom-call(s32[3]{0:T(128)} %pad_add_fusion.where, s32[64]{0:T(128)} %reshape.20.union, f32[1,256,1024]{2,1,0:T(8,128)} %collective-permute-done.19.refs_0_, f32[1,128,1024]{2,1,0:T(8,128)} %collective-permute-done.20.refs_1_, ...), custom_call_target="tpu_custom_call" | custom-call | flops 603979776 | bytes 15728640 | tf_op jit(solution)/shard_map/density_rows/pallas_call | solution.py:295
  223.5 2.1 potential_net.1.refs_8_
  228.6 5.9 %potential_rows.7 = (f32[128,1024]{1,0:T(8,128)S(1)}, f32[128,2048]{1,0:T(8,128)S(1)}, f32[128,1024]{1,0:T(8,128)S(1)}, f32[128,1024]{1,0:T(8,128)S(1)}, f32[128...) custom-call(s32[3]{0:T(128)S(1)} %copy-done.6, s32[64]{0:T(128)S(1)} %copy-done.8, bf16[2,384,1024]{2,1,0:T(8,128)(2,1)S(1)} %copy-done, ...), custom_call_target="tpu_custom_call" | custom-call | flops 3221225472 | bytes 16777216 | tf_op jit(solution)/shard_map/potential_rows/pallas_call | solution.py:330
  234.5 5.2 %collective-permute-start.31 = (f32[128,2048]{1,0:T(8,128)S(1)}, f32[128,2048]{1,0:T(8,128)S(1)}, u32[]{:S(2)}, u32[]{:S(2)}) collective-permute-start(f32[128,2048]{1,0:T(8,128)S(1)} %get-tuple-element.55), channel_id=1, source_target_pairs={{0,8},{8,16},{16,24},{1,9},{9,17},{17,25},{2,10},{10,18},{18,26},{... | collective-permute-start | bytes 3145736 | tf_op jit(solution)/shard_map/ppermute | solution.py:444
  241.5 7.8 %potential_rows.5 = (f32[128,1024]{1,0:T(8,128)S(1)}, f32[128,2048]{1,0:T(8,128)S(1)}, f32[128,1024]{1,0:T(8,128)S(1)}, f32[128,1024]{1,0:T(8,128)S(1)}, f32[128...) custom-call(s32[3]{0:T(128)S(1)} %copy-done.6, s32[64]{0:T(128)S(1)} %copy-done.8, bf16[2,384,1024]{2,1,0:T(8,128)(2,1)S(1)} %copy-done, ...), custom_call_target="tpu_custom_call" | custom-call | flops 3221225472 | bytes 16777216 | tf_op jit(solution)/shard_map/potential_rows/pallas_call | solution.py:330
  251.3 6.0 %collective-permute-start.34 = (f32[128,1024]{1,0:T(8,128)S(1)}, f32[128,1024]{1,0:T(8,128)}, u32[]{:S(2)}, u32[]{:S(2)}) collective-permute-start(f32[128,1024]{1,0:T(8,128)S(1)} %get-tuple-element.58), channel_id=1, source_target_pairs={{0,8},{8,16},{1,9},{9,17},{2,10},{10,18},{3,11},{11,19},{4,12},{12... | collective-permute-start | bytes 1572872 | tf_op jit(solution)/shard_map/ppermute | solution.py:444
  257.2 5.5 %potential_rows.6 = (f32[128,1024]{1,0:T(8,128)S(1)}, f32[128,2048]{1,0:T(8,128)S(1)}, f32[128,1024]{1,0:T(8,128)S(1)}) custom-call(s32[3]{0:T(128)S(1)} %copy-done.6, s32[64]{0:T(128)S(1)} %copy-done.8, bf16[2,384,1024]{2,1,0:T(8,128)(2,1)S(1)} %copy-done, bf16[2,384,1024]{2,1,0:T(8,128)(2,1)S(1)} %copy-done.1, ...), custom_call_target="tpu_custom_call" | custom-call | flops 1610612736 | bytes 14680064 | tf_op jit(solution)/shard_map/potential_rows/pallas_call | solution.py:330
  265.5 2.4 add_add_fusion
  269.2 5.7 %collective-permute-start.27 = (f32[128,1024]{1,0:T(8,128)S(1)}, f32[128,1024]{1,0:T(8,128)S(1)}, u32[]{:S(2)}, u32[]{:S(2)}) collective-permute-start(f32[128,1024]{1,0:T(8,128)S(1)} %get-tuple-element.50), channel_id=1, source_target_pairs={{0,8},{8,16},{1,9},{9,17},{2,10},{10,18},{3,11},{11,19},{4,12},{12... | collective-permute-start | bytes 1572872 | tf_op jit(solution)/shard_map/ppermute | solution.py:444
  274.9 4.3 %collective-permute-start.28 = (f32[128,2048]{1,0:T(8,128)S(1)}, f32[128,2048]{1,0:T(8,128)S(1)}, u32[]{:S(2)}, u32[]{:S(2)}) collective-permute-start(f32[128,2048]{1,0:T(8,128)S(1)} %get-tuple-element.51), channel_id=1, source_target_pairs={{0,8},{8,16},{16,24},{1,9},{9,17},{17,25},{2,10},{10,18},{18,26},{... | collective-permute-start | bytes 3145736 | tf_op jit(solution)/shard_map/ppermute | solution.py:444
  281.7 4.5 %collective-permute-start.35 = (f32[128,1024]{1,0:T(8,128)S(1)}, f32[128,1024]{1,0:T(8,128)S(1)}, u32[]{:S(2)}, u32[]{:S(2)}) collective-permute-start(f32[128,1024]{1,0:T(8,128)S(1)} %add_add_fusion.2), channel_id=1, source_target_pairs={{0,4},{1,5},{2,6},{3,7},{4,0},{5,1},{6,2},{7,3},{8,12},{9,13},{10,... | collective-permute-start | bytes 1572872 | tf_op jit(solution)/shard_map/ppermute | solution.py:452
  286.9 6.4 %potential_rows.4 = (f32[128,1024]{1,0:T(8,128)S(1)}, f32[128,2048]{1,0:T(8,128)S(1)}, f32[128,1024]{1,0:T(8,128)S(1)}) custom-call(s32[3]{0:T(128)S(1)} %copy-done.6, s32[64]{0:T(128)S(1)} %copy-done.8, bf16[2,384,1024]{2,1,0:T(8,128)(2,1)S(1)} %copy-done, bf16[2,384,1024]{2,1,0:T(8,128)(2,1)S(1)} %copy-done.1, ...), custom_call_target="tpu_custom_call" | custom-call | flops 1610612736 | bytes 14680064 | tf_op jit(solution)/shard_map/potential_rows/pallas_call | solution.py:330
  294.5 2.0 joined_rows.1.sum_ref
  296.5 50.0 %collective-permute-done.32.term_ref = f32[128,2048]{1,0:T(8,128)S(1)} collective-permute-done((f32[128,2048]{1,0:T(8,128)}, f32[128,2048]{1,0:T(8,128)S(1)}, u32[]{:S(2)}, u32[]{:S(2)}) %collective-permute-start.32) | collective-permute-done | bytes 1048608 | tf_op jit(solution)/shard_map/ppermute | solution.py:452
  346.5 2.1 added_rows.3.sum_ref
  348.5 9.2 %collective-permute-done.35.term_ref = f32[128,1024]{1,0:T(8,128)S(1)} collective-permute-done((f32[128,1024]{1,0:T(8,128)S(1)}, f32[128,1024]{1,0:T(8,128)S(1)}, u32[]{:S(2)}, u32[]{:S(2)}) %collective-permute-start.35) | collective-permute-done | bytes 524320 | tf_op jit(solution)/shard_map/ppermute | solution.py:452
  357.7 1.9 added_rows.4.sum_ref
  359.6 1.9 added_rows.5
  (152 shorter events, 55.2 us)
Async XLA Ops:
  2.1 97.6 %collective-permute-start.16 = (f32[1,256,1024]{2,1,0:T(8,128)S(1)}, f32[1,256,1024]{2,1,0:T(8,128)}, u32[]{:S(2)}, u32[]{:S(2)}) collective-permute-start(f32[1,256,1024]{2,1,0:T(8,128)S(1)} %slice.35), channel_id=1, source_target_pairs={{0,2},{1,3},{2,0},{3,1},{4,6},{5,7},{6,4},{7,5},{8,10},{9,11},{10,... | collective-permute-start | bytes 3145736 | tf_op jit(solution)/shard_map/ppermute | solution.py:426
  5.2 150.4 %collective-permute-start.5 = (f32[2,384,1024]{2,1,0:T(8,128)}, f32[2,384,1024]{2,1,0:T(8,128)S(1)}, u32[]{:S(2)}, u32[]{:S(2)}) collective-permute-start(f32[2,384,1024]{2,1,0:T(8,128)} %refs_0_.3), channel_id=1, source_target_pairs={{0,1},{1,0},{2,3},{3,2},{4,5},{5,4},{6,7},{7,6},{8,9},{9,8},{10,11... | collective-permute-start | bytes 9437192 | tf_op jit(solution)/shard_map/ppermute | solution.py:426
  6.8 68.7 %collective-permute-start.7 = (f32[128,1024]{1,0:T(8,128)S(1)}, f32[128,1024]{1,0:T(8,128)S(1)}, u32[]{:S(2)}, u32[]{:S(2)}) collective-permute-start(f32[128,1024]{1,0:T(8,128)S(1)} %get-tuple-element.63), channel_id=1, source_target_pairs={{0,4},{1,5},{2,6},{3,7},{4,0},{5,1},{6,2},{7,3},{8,12},{9,13},{10,... | collective-permute-start | bytes 1572872 | tf_op jit(solution)/shard_map/ppermute | solution.py:452
  11.7 29.3 %collective-permute-start.4 = (f32[2,512]{1,0:T(2,128)S(1)}, f32[2,512]{1,0:T(2,128)S(1)}, u32[]{:S(2)}, u32[]{:S(2)}) collective-permute-start(f32[2,512]{1,0:T(2,128)S(1)} %select_maximum_fusion), channel_id=1, source_target_pairs={{0,3},{1,2},{2,1},{3,0},{4,7},{5,6},{6,5},{7,4},{8,11},{9,10},{10,... | collective-permute-start | bytes 12296 | tf_op jit(solution)/shard_map/ppermute | solution.py:426
  12.1 29.2 %collective-permute-start.3 = (f32[2,512]{1,0:T(2,128)S(1)}, f32[2,512]{1,0:T(2,128)S(1)}, u32[]{:S(2)}, u32[]{:S(2)}) collective-permute-start(f32[2,512]{1,0:T(2,128)S(1)} %select_maximum_fusion), channel_id=1, source_target_pairs={{0,2},{1,3},{2,0},{3,1},{4,6},{5,7},{6,4},{7,5},{8,10},{9,11},{10,... | collective-permute-start | bytes 12296 | tf_op jit(solution)/shard_map/ppermute | solution.py:426
  40.9 34.2 %collective-permute-start.2 = (f32[2,512]{1,0:T(2,128)S(1)}, f32[2,512]{1,0:T(2,128)S(1)}, u32[]{:S(2)}, u32[]{:S(2)}) collective-permute-start(f32[2,512]{1,0:T(2,128)S(1)} %select_maximum_fusion), channel_id=1, source_target_pairs={{0,1},{1,0},{2,3},{3,2},{4,5},{5,4},{6,7},{7,6},{8,9},{9,8},{10,11... | collective-permute-start | bytes 12296 | tf_op jit(solution)/shard_map/ppermute | solution.py:426
  41.3 35.7 %collective-permute-start.11 = (f32[128,1024]{1,0:T(8,128)S(1)}, f32[128,1024]{1,0:T(8,128)}, u32[]{:S(2)}, u32[]{:S(2)}) collective-permute-start(f32[128,1024]{1,0:T(8,128)S(1)} %get-tuple-element.62), channel_id=1, source_target_pairs={{8,12},{9,13},{10,14},{11,15},{12,8},{13,9},{14,10},{15,11},{16,20... | collective-permute-start | bytes 1572872 | tf_op jit(solution)/shard_map/ppermute | solution.py:452
  75.2 23.1 %collective-permute-start.17 = (f32[1,128,1024]{2,1,0:T(8,128)S(1)}, f32[1,128,1024]{2,1,0:T(8,128)S(1)}, u32[]{:S(2)}, u32[]{:S(2)}) collective-permute-start(f32[1,128,1024]{2,1,0:T(8,128)S(1)} %slice.36), channel_id=1, source_target_pairs={{0,2},{1,3},{2,0},{3,1},{4,6},{5,7},{6,4},{7,5},{8,10},{9,11},{10,... | collective-permute-start | bytes 1572872 | tf_op jit(solution)/shard_map/ppermute | solution.py:426
  75.5 24.2 %collective-permute-start.8 = (f32[128,1024]{1,0:T(8,128)S(1)}, f32[128,1024]{1,0:T(8,128)S(1)}, u32[]{:S(2)}, u32[]{:S(2)}) collective-permute-start(f32[128,1024]{1,0:T(8,128)S(1)} %collective-permute-done.7.refs_6_.refs_9_.refs_8_), channel_id=1, source_target_pairs={{0,8},{1,9},{2,10},{3,11},{4,12},{5,13},{6,14},{7,15}} | collective-permute-start | bytes 1572872 | tf_op jit(solution)/shard_map/ppermute | solution.py:444
  77.0 47.3 %collective-permute-start.9 = (f32[128,2048]{1,0:T(8,128)S(1)}, f32[128,2048]{1,0:T(8,128)S(1)}, u32[]{:S(2)}, u32[]{:S(2)}) collective-permute-start(f32[128,2048]{1,0:T(8,128)S(1)} %slice.33), channel_id=1, source_target_pairs={{0,4},{1,5},{2,6},{3,7},{4,0},{5,1},{6,2},{7,3},{8,12},{9,13},{10,... | collective-permute-start | bytes 3145736 | tf_op jit(solution)/shard_map/ppermute | solution.py:452
  98.2 54.7 %collective-permute-start = (f32[128,4096]{1,0:T(8,128)S(1)}, f32[128,4096]{1,0:T(8,128)S(1)}, u32[]{:S(2)}, u32[]{:S(2)}) collective-permute-start(f32[128,4096]{1,0:T(8,128)S(1)} %copy-done.9), channel_id=1, source_target_pairs={{0,8},{8,16},{16,24},{1,9},{9,17},{17,25},{2,10},{10,18},{18,26},{... | collective-permute-start | bytes 6291464 | tf_op jit(solution)/shard_map/ppermute | solution.py:23
  99.7 47.4 %collective-permute-start.6 = (f32[1,384,1024]{2,1,0:T(8,128)S(1)}, f32[1,384,1024]{2,1,0:T(8,128)}, u32[]{:S(2)}, u32[]{:S(2)}) collective-permute-start(f32[1,384,1024]{2,1,0:T(8,128)S(1)} %slice.31), channel_id=1, source_target_pairs={{0,2},{1,3},{2,0},{3,1},{4,6},{5,7},{6,4},{7,5},{8,10},{9,11},{10,... | collective-permute-start | bytes 4718600 | tf_op jit(solution)/shard_map/ppermute | solution.py:426
  99.8 54.5 %collective-permute-start.1 = (f32[128,4096]{1,0:T(8,128)S(1)}, f32[128,4096]{1,0:T(8,128)S(1)}, u32[]{:S(2)}, u32[]{:S(2)}) collective-permute-start(f32[128,4096]{1,0:T(8,128)S(1)} %copy-done.9), channel_id=1, source_target_pairs={{8,0},{16,8},{24,16},{9,1},{17,9},{25,17},{10,2},{18,10},{26,18},{... | collective-permute-start | bytes 6291464 | tf_op jit(solution)/shard_map/ppermute | solution.py:23
  125.1 23.7 %collective-permute-start.13 = (f32[128,1024]{1,0:T(8,128)S(1)}, f32[128,1024]{1,0:T(8,128)S(1)}, u32[]{:S(2)}, u32[]{:S(2)}) collective-permute-start(f32[128,1024]{1,0:T(8,128)S(1)} %collective-permute-done.7.refs_6_.refs_9_.refs_8_), channel_id=1, source_target_pairs={{8,0},{16,8},{9,1},{17,9},{10,2},{18,10},{11,3},{19,11},{12,4},{20... | collective-permute-start | bytes 1572872 | tf_op jit(solution)/shard_map/ppermute | solution.py:444
  147.1 36.8 %collective-permute-start.18 = (f32[1,384,1024]{2,1,0:T(8,128)}, f32[1,384,1024]{2,1,0:T(8,128)}, u32[]{:S(2)}, u32[]{:S(2)}) collective-permute-start(f32[1,384,1024]{2,1,0:T(8,128)} %collective-permute-done.6.refs_1_.refs_2_), channel_id=1, source_target_pairs={{0,1},{1,0},{2,3},{3,2},{4,5},{5,4},{6,7},{7,6},{8,9},{9,8},{10,11... | collective-permute-start | bytes 4718600 | tf_op jit(solution)/shard_map/ppermute | solution.py:426
  148.8 30.7 %collective-permute-start.10 = (f32[128,2048]{1,0:T(8,128)S(1)}, f32[128,2048]{1,0:T(8,128)}, u32[]{:S(2)}, u32[]{:S(2)}) collective-permute-start(f32[128,2048]{1,0:T(8,128)S(1)} %collective-permute-done.9.refs_7_.refs_10_.refs_9_), channel_id=1, source_target_pairs={{0,8},{8,16},{16,24},{1,9},{9,17},{17,25},{2,10},{10,18},{18,26},{... | collective-permute-start | bytes 3145736 | tf_op jit(solution)/shard_map/ppermute | solution.py:444
  153.0 26.5 %collective-permute-start.14 = (f32[128,2048]{1,0:T(8,128)S(1)}, f32[128,2048]{1,0:T(8,128)}, u32[]{:S(2)}, u32[]{:S(2)}) collective-permute-start(f32[128,2048]{1,0:T(8,128)S(1)} %collective-permute-done.9.refs_7_.refs_10_.refs_9_), channel_id=1, source_target_pairs={{8,0},{16,8},{24,16},{9,1},{17,9},{25,17},{10,2},{18,10},{26,18},{... | collective-permute-start | bytes 3145736 | tf_op jit(solution)/shard_map/ppermute | solution.py:444
  154.3 16.0 %collective-permute-start.15 = (f32[128,1024]{1,0:T(8,128)}, f32[128,1024]{1,0:T(8,128)S(1)}, u32[]{:S(2)}, u32[]{:S(2)}) collective-permute-start(f32[128,1024]{1,0:T(8,128)} %collective-permute-done.11.refs_8_.refs_11_.refs_10_), channel_id=1, source_target_pairs={{24,16},{25,17},{26,18},{27,19},{28,20},{29,21},{30,22},{31,23}} | collective-permute-start | bytes 1572872 | tf_op jit(solution)/shard_map/ppermute | solution.py:444
  157.3 49.1 %collective-permute-start.19 = (f32[1,256,1024]{2,1,0:T(8,128)}, f32[1,256,1024]{2,1,0:T(8,128)}, u32[]{:S(2)}, u32[]{:S(2)}) collective-permute-start(f32[1,256,1024]{2,1,0:T(8,128)} %collective-permute-done.16.refs_0_), channel_id=1, source_target_pairs={{0,1},{1,0},{2,3},{3,2},{4,5},{5,4},{6,7},{7,6},{8,9},{9,8},{10,11... | collective-permute-start | bytes 3145736 | tf_op jit(solution)/shard_map/ppermute | solution.py:426
  170.3 36.0 %collective-permute-start.20 = (f32[1,128,1024]{2,1,0:T(8,128)}, f32[1,128,1024]{2,1,0:T(8,128)}, u32[]{:S(2)}, u32[]{:S(2)}) collective-permute-start(f32[1,128,1024]{2,1,0:T(8,128)} %slice.40), channel_id=1, source_target_pairs={{0,2},{1,3},{2,0},{3,1},{4,6},{5,7},{6,4},{7,5},{8,10},{9,11},{10,... | collective-permute-start | bytes 1572872 | tf_op jit(solution)/shard_map/ppermute | solution.py:426
  234.5 29.6 %collective-permute-start.31 = (f32[128,2048]{1,0:T(8,128)S(1)}, f32[128,2048]{1,0:T(8,128)S(1)}, u32[]{:S(2)}, u32[]{:S(2)}) collective-permute-start(f32[128,2048]{1,0:T(8,128)S(1)} %get-tuple-element.55), channel_id=1, source_target_pairs={{0,8},{8,16},{16,24},{1,9},{9,17},{17,25},{2,10},{10,18},{18,26},{... | collective-permute-start | bytes 3145736 | tf_op jit(solution)/shard_map/ppermute | solution.py:444
  239.7 25.1 %collective-permute-start.30 = (f32[128,2048]{1,0:T(8,128)S(1)}, f32[128,2048]{1,0:T(8,128)}, u32[]{:S(2)}, u32[]{:S(2)}) collective-permute-start(f32[128,2048]{1,0:T(8,128)S(1)} %get-tuple-element.54), channel_id=1, source_target_pairs={{8,0},{16,8},{24,16},{9,1},{17,9},{25,17},{10,2},{18,10},{26,18},{... | collective-permute-start | bytes 3145736 | tf_op jit(solution)/shard_map/ppermute | solution.py:444
  249.3 13.5 %collective-permute-start.24 = (f32[128,1024]{1,0:T(8,128)S(1)}, f32[128,1024]{1,0:T(8,128)S(1)}, u32[]{:S(2)}, u32[]{:S(2)}) collective-permute-start(f32[128,1024]{1,0:T(8,128)S(1)} %get-tuple-element.47), channel_id=1, source_target_pairs={{8,0},{9,1},{10,2},{11,3},{12,4},{13,5},{14,6},{15,7}} | collective-permute-start | bytes 1572872 | tf_op jit(solution)/shard_map/ppermute | solution.py:444
  250.6 17.4 %collective-permute-start.26 = (f32[128,1024]{1,0:T(8,128)S(1)}, f32[128,1024]{1,0:T(8,128)S(1)}, u32[]{:S(2)}, u32[]{:S(2)}) collective-permute-start(f32[128,1024]{1,0:T(8,128)S(1)} %get-tuple-element.49), channel_id=1, source_target_pairs={{16,8},{24,16},{17,9},{25,17},{18,10},{26,18},{19,11},{27,19},{20,... | collective-permute-start | bytes 1572872 | tf_op jit(solution)/shard_map/ppermute | solution.py:444
  251.3 17.9 %collective-permute-start.34 = (f32[128,1024]{1,0:T(8,128)S(1)}, f32[128,1024]{1,0:T(8,128)}, u32[]{:S(2)}, u32[]{:S(2)}) collective-permute-start(f32[128,1024]{1,0:T(8,128)S(1)} %get-tuple-element.58), channel_id=1, source_target_pairs={{0,8},{8,16},{1,9},{9,17},{2,10},{10,18},{3,11},{11,19},{4,12},{12... | collective-permute-start | bytes 1572872 | tf_op jit(solution)/shard_map/ppermute | solution.py:444
  264.1 15.1 %collective-permute-start.37 = (f32[128,1024]{1,0:T(8,128)S(1)}, f32[128,1024]{1,0:T(8,128)S(1)}, u32[]{:S(2)}, u32[]{:S(2)}) collective-permute-start(f32[128,1024]{1,0:T(8,128)S(1)} %get-tuple-element.61), channel_id=1, source_target_pairs={{16,24},{17,25},{18,26},{19,27},{20,28},{21,29},{22,30},{23,31}} | collective-permute-start | bytes 1572872 | tf_op jit(solution)/shard_map/ppermute | solution.py:444
  264.8 15.1 %collective-permute-start.36 = (f32[128,1024]{1,0:T(8,128)S(1)}, f32[128,1024]{1,0:T(8,128)S(1)}, u32[]{:S(2)}, u32[]{:S(2)}) collective-permute-start(f32[128,1024]{1,0:T(8,128)S(1)} %get-tuple-element.60), channel_id=1, source_target_pairs={{16,8},{24,16},{17,9},{25,17},{18,10},{26,18},{19,11},{27,19},{20,... | collective-permute-start | bytes 1572872 | tf_op jit(solution)/shard_map/ppermute | solution.py:444
  267.9 26.6 %collective-permute-start.25 = (f32[128,2048]{1,0:T(8,128)S(1)}, f32[128,2048]{1,0:T(8,128)S(1)}, u32[]{:S(2)}, u32[]{:S(2)}) collective-permute-start(f32[128,2048]{1,0:T(8,128)S(1)} %get-tuple-element.48), channel_id=1, source_target_pairs={{8,0},{16,8},{24,16},{9,1},{17,9},{25,17},{10,2},{18,10},{26,18},{... | collective-permute-start | bytes 3145736 | tf_op jit(solution)/shard_map/ppermute | solution.py:444
  274.9 19.6 %collective-permute-start.28 = (f32[128,2048]{1,0:T(8,128)S(1)}, f32[128,2048]{1,0:T(8,128)S(1)}, u32[]{:S(2)}, u32[]{:S(2)}) collective-permute-start(f32[128,2048]{1,0:T(8,128)S(1)} %get-tuple-element.51), channel_id=1, source_target_pairs={{0,8},{8,16},{16,24},{1,9},{9,17},{17,25},{2,10},{10,18},{18,26},{... | collective-permute-start | bytes 3145736 | tf_op jit(solution)/shard_map/ppermute | solution.py:444
  279.9 66.5 %collective-permute-start.32 = (f32[128,2048]{1,0:T(8,128)}, f32[128,2048]{1,0:T(8,128)S(1)}, u32[]{:S(2)}, u32[]{:S(2)}) collective-permute-start(f32[128,2048]{1,0:T(8,128)} %add_add_fusion), channel_id=1, source_target_pairs={{0,4},{1,5},{2,6},{3,7},{4,0},{5,1},{6,2},{7,3},{8,12},{9,13},{10,... | collective-permute-start | bytes 3145736 | tf_op jit(solution)/shard_map/ppermute | solution.py:452
  281.7 76.0 %collective-permute-start.35 = (f32[128,1024]{1,0:T(8,128)S(1)}, f32[128,1024]{1,0:T(8,128)S(1)}, u32[]{:S(2)}, u32[]{:S(2)}) collective-permute-start(f32[128,1024]{1,0:T(8,128)S(1)} %add_add_fusion.2), channel_id=1, source_target_pairs={{0,4},{1,5},{2,6},{3,7},{4,0},{5,1},{6,2},{7,3},{8,12},{9,13},{10,... | collective-permute-start | bytes 1572872 | tf_op jit(solution)/shard_map/ppermute | solution.py:452
  286.2 73.5 %collective-permute-start.38 = (f32[128,1024]{1,0:T(8,128)S(1)}, f32[128,1024]{1,0:T(8,128)S(1)}, u32[]{:S(2)}, u32[]{:S(2)}) collective-permute-start(f32[128,1024]{1,0:T(8,128)S(1)} %add_add_fusion.1), channel_id=1, source_target_pairs={{8,12},{9,13},{10,14},{11,15},{12,8},{13,9},{14,10},{15,11},{16,20... | collective-permute-start | bytes 1572872 | tf_op jit(solution)/shard_map/ppermute | solution.py:452
  (40 other events, 1356.6 us)
